TPU v7x, 256 devices: a whole 4x4x8 slice. The times are simulated.
256 devices in a mesh: dom: 64 (over x_lo, z, y), orb: 4 (over x_hi, core).
Axes of the slice: x: 4 (x_hi: 2, x_lo: 2; x = x_hi * 2 + x_lo), y: 4, z: 8, core: 2. Of those that a mesh axis runs over, the one named last changes fastest.
Arguments:
- orbitals: bfloat16 [128, 4, 1024, 512], P('dom', None, None, 'orb'), may hold values from -6 to 6
- slot_ids: int32 [128, 4], P('dom'), may hold values from 0 to 15, as said below
- slot_count: int32 [128], P('dom'), may hold values from 1 to 4, as said below
- band_tiles: bfloat16 [16, 3, 512, 512], P(None, None, 'dom', 'orb'), may hold values from -0.15625 to 0.15625
- pattern: int32 [16, 3], replicated, may hold values 0 or 1
- occupation: float32 [16, 512], P(None, 'orb'), may hold values from 0.0005 to 0.005
Outputs:
- rotated: bfloat16 [128, 4, 1024, 512], P('dom', None, None, 'orb')
- density: float32 [128, 1024], P('dom')
Inputs may be any that keep to these rules, and one draw needn't show every extreme that they name: `slot_ids`: each row names 4 consecutive orbital blocks counted modulo 16: slot l holds (s + l) mod 16, where the first block s of a grid block may be any of the 16 blocks. The slots in use on grid block g are its first slot_count[g]; some grid block uses all 4.
All inputs are finite; a program needn't handle non-finite values.
Results may differ from a plain program's by a relative error of at most 0.00094.
Values may be sent and summed in bfloat16 or wider, within the bound.
A program may use at most 128 MiB of HBM per device.

v0:
```python
import jax
import jax.numpy as jnp
from jax import lax
from jax.sharding import Mesh
from jax.sharding import PartitionSpec as P

DOM = ("dom_0", "dom_1", "dom_2")


def laid_out(tiles, dim):
    shape = list(tiles.shape[1:])
    shape[dim] *= tiles.shape[0]
    return jnp.moveaxis(tiles, 0, dim).reshape(shape)


def all_blocks(x, axes, sequence):
    tiles = x
    for k in sequence:
        tiles = lax.all_gather(tiles, axes[k])
    done = sequence[::-1]
    back = [done.index(k) for k in range(len(axes))]
    tiles = tiles.transpose(*back, *range(len(axes), tiles.ndim))
    return tiles.reshape(-1, *x.shape)


def whole_of(x, axes, sequence, dim):
    return laid_out(all_blocks(x, axes, sequence), dim)


def from_everyone(x, axis):
    peers = lax.axis_size(axis)
    return lax.all_to_all(jnp.broadcast_to(x[None], (peers, *x.shape)), axis, 0, 0, tiled=True)


def of_everyone(x, axis):
    return from_everyone(x, axis).sum(axis=0)


def select_tiles(band_full, pattern, slot_ids, slot_count):
    slots_per = slot_ids.shape[1]
    band_count = pattern.shape[1]
    half_band = (band_count - 1) // 2
    active = jnp.arange(slots_per, dtype=jnp.int32)[None, :] < slot_count[:, None]
    source = slot_ids[:, :, None]
    target = slot_ids[:, None, :]
    offset = target - source + half_band
    inside = (offset >= 0) & (offset < band_count)
    column = jnp.clip(offset, 0, band_count - 1)
    keeping = inside & (pattern[source, column] == 1) & active[:, :, None] & active[:, None, :]
    picked = band_full[source, column]
    return jnp.where(keeping[:, :, :, None, None], picked, jnp.zeros((), picked.dtype))


def rotate(values, tile_set):
    return jnp.einsum("glpi,glmij->gmpj", values, tile_set, preferred_element_type=jnp.float32)


def local(orbitals, slot_ids, slot_count, band_tiles, pattern, occupation):
    all_rows = whole_of(band_tiles, DOM, (0, 1, 2), 2)
    tile_set = select_tiles(all_rows, pattern, slot_ids, slot_count)
    rotated_f = rotate(lax.all_gather(orbitals, "orb", axis=3, tiled=True), tile_set)
    rotated = rotated_f.astype(jnp.bfloat16)
    onehot = (
        slot_ids[:, :, None] == jnp.arange(occupation.shape[0], dtype=jnp.int32)[None, None, :]
    ).astype(jnp.float32)
    weights = jnp.einsum("glb,bj->glj", onehot, occupation, precision=lax.Precision.HIGHEST)
    widened = rotated.astype(jnp.float32)
    square = widened * widened
    partial_density = jnp.einsum("gmpj,gmj->gp", square, weights, precision=lax.Precision.HIGHEST)
    density = of_everyone(partial_density, "orb")
    return (rotated, density)


def solution(mesh):
    torus = Mesh(
        mesh.devices.reshape(2, 8, 4, mesh.shape["orb"]), ("dom_0", "dom_1", "dom_2", "orb")
    )
    return jax.shard_map(
        local,
        mesh=torus,
        in_specs=(
            P(DOM, None, None, "orb"),
            P(DOM, None),
            P(DOM),
            P(None, None, DOM, "orb"),
            P(),
            P(None, "orb"),
        ),
        out_specs=(P(DOM, None, None, "orb"), P(DOM, None)),
        check_vma=False,
    )
```

profile of v0, /device:TPU:1, one launch (start us, length us, event | category | flops | bytes accessed | tf_op | source)
XLA Modules:
  0.0 223.0 jit_solution(2459626745871815533)
XLA Ops:
  7.2 0.0 copy-start
  7.2 0.0 copy-start.2
  7.2 0.0 copy-start.1
  7.2 0.0 copy-start.3
  7.2 0.0 all-gather.9.cloned.1.call-start
  7.3 6.5 %all-gather = bf16[32,3,8,128]{3,2,1,0:T(8,128)(2,1)} all-gather(bf16[16,3,8,128]{3,2,1,0:T(8,128)(2,1)} %param.9), channel_id=2, replica_groups=mesh['dom_0'=2,'dom_1'=8,'dom_2'=4,'orb'=4] {'dom_0'}, dimensions={0}, use_global_device_ids=true | all-gather | bytes 294912 | tf_op jit(solution)/shard_map/all_gather | solution.py:19
  13.7 0.0 all-gather.9.cloned.1.call-update
  13.8 0.0 all-gather.11.cloned.1.call-start
  13.8 39.6 %all-gather.9.cloned.1.call-done = bf16[16,16,3,8,128]{4,3,2,1,0:T(8,128)(2,1)} async-done(((bf16[2,16,3,8,128]{4,3,2,1,0:T(8,128)(2,1)}), bf16[16,16,3,8,128]{4,3,2,1,0:T(8,128)(2,1)}) %all-gather.9.cloned.1.call-update) | async-done | bytes 1572880 | tf_op jit(solution)/shard_map/all_gather | solution.py:19
  53.4 0.0 all-gather.11.cloned.1.call-update
  53.4 0.0 all-gather.7.cloned.1.call-start
  53.5 0.7 all-gather.7.cloned.1.call-update
  54.2 0.7 fusion.26
  54.8 0.8 fusion.17
  55.7 0.1 reshape.85
  55.8 0.8 gather_fusion
  56.5 0.1 reshape.101
  56.6 0.1 iota_compare_fusion.2
  56.7 0.1 fusion.23
  56.8 0.2 fusion.13
  57.0 68.7 %all-gather.11.cloned.1.call-done = bf16[32,2,16,3,8,128]{5,4,3,2,1,0:T(8,128)(2,1)} async-done(((bf16[8,2,16,3,8,128]{5,4,3,2,1,0:T(8,128)(2,1)}), bf16[32,2,16,3,8,128]{5,4,3,2,1,0:T(8,128)(2,1)}) %all-gather.11.cloned.1.call-update) | async-done | bytes 6291472 | tf_op jit(solution)/shard_map/all_gather | solution.py:19
  125.7 3.9 %copy.25 = bf16[2,8,4,16,3,8,128]{6,5,4,3,2,1,0:T(8,128)(2,1)S(1)} copy(bf16[2,8,4,16,3,8,128]{6,5,4,3,0,1,2:T(8,128)(2,1)} %bitcast.43) | data formatting | bytes 12582912 | tf_op jit(solution)/shard_map/transpose | solution.py:22
  129.6 4.9 %copy_bitcast_fusion = bf16[16,3,512,128]{3,2,1,0:T(8,128)(2,1)} fusion(bf16[2,8,4,16,3,8,128]{6,5,4,3,2,1,0:T(8,128)(2,1)S(1)} %copy.25), kind=kLoop, calls=%fused_computation.4 | loop fusion | bytes 12582912 | tf_op jit(solution)/shard_map/reshape | solution.py:13
  134.5 5.8 %gather_fusion.1 = bf16[32,512,128]{2,1,0:T(8,128)(2,1)} fusion(bf16[16,3,512,128]{3,2,1,0:T(8,128)(2,1)} %copy_bitcast_fusion, s32[32]{0:T(128)S(1)} %reshape.85), kind=kCustom, calls=%fused_computation.1 | custom fusion | bytes 8388864 | tf_op jit(solution)/shard_map/gather | solution.py:50
  140.3 54.4 %all-gather.7.cloned.1.call-done = bf16[2,4,1024,512]{3,2,1,0:T(8,128)(2,1)} async-done(((bf16[2,4,1024,128]{3,2,1,0:T(8,128)(2,1)}), bf16[2,4,1024,512]{3,2,1,0:T(8,128)(2,1)}) %all-gather.7.cloned.1.call-update) | async-done | bytes 8388624 | tf_op jit(solution)/shard_map/all_gather | solution.py:61
  194.7 9.8 %fusion.7 = bf16[2,4,1024,128]{2,3,1,0:T(8,128)(2,1)S(1)} fusion(bf16[2,4,1024,512]{3,2,1,0:T(8,128)(2,1)} %all-gather.7.cloned.1.call-done, bf16[2,4,4,512,128]{4,3,2,1,0:T(8,128)(2,1)} %bitcast.44, pred[2,4,4]{2,1,0:T(4,128)(4,1)S(1)} %fusion.23), kind=kOutput, calls=%fused_computation.11 | convolution fusion | flops 4298113024 | bytes 14680096 | tf_op jit(solution)/shard_map/glpi,glmij->gmpj/dot_general | solution.py:55
  204.6 2.5 %fusion.2 = f32[2,1,1024,1]{2,1,3,0:T(1,128)S(1)} fusion(f32[2,4,128,1]{2,3,1,0:T(1,128)S(1)} %bitcast.48, bf16[2,4,1024,128]{2,3,1,0:T(8,128)(2,1)S(1)} %fusion.7), kind=kOutput, calls=%fused_computation.6 | convolution fusion | flops 14680064 | bytes 2109440 | tf_op jit(solution)/shard_map/gmpj,gmj->gp/dot_general | solution.py:69
  207.1 0.6 broadcast_in_dim.15
  207.7 3.5 %all-to-all-start = ((f32[4,2,1024]{2,1,0:T(2,128)}), f32[4,2,1024]{2,1,0:T(2,128)S(1)}, u32[]{:S(2)}, u32[]{:S(2)}) async-start(f32[4,2,1024]{2,1,0:T(2,128)} %broadcast_in_dim.15), calls=%async_computation | async-start | bytes 65536 | tf_op jit(solution)/shard_map/all_to_all | solution.py:32
  211.2 2.5 %copy.29 = bf16[2,4,1024,128]{3,2,1,0:T(8,128)(2,1)} copy(bf16[2,4,1024,128]{2,3,1,0:T(8,128)(2,1)S(1)} %fusion.7) | data formatting | bytes 4194304
  213.7 2.1 all-to-all-done
  215.9 0.6 reduce_sum.9
  (6 shorter events, 0.0 us)
Async XLA Ops:
  7.2 49.6 %copy-start = (f32[16,128]{1,0:T(8,128)S(1)}, f32[16,128]{1,0:T(8,128)}, u32[]{:S(2)}) copy-start(f32[16,128]{1,0:T(8,128)} %param.11) | copy-start | bytes 24580
  7.2 49.5 %copy-start.2 = (s32[2,4]{1,0:T(2,128)S(1)}, s32[2,4]{1,0:T(2,128)}, u32[]{:S(2)}) copy-start(s32[2,4]{1,0:T(2,128)} %param.7) | copy-start | bytes 100
  7.2 48.6 %copy-start.1 = (s32[16,3]{0,1:T(4,128)S(1)}, s32[16,3]{0,1:T(4,128)}, u32[]{:S(2)}) copy-start(s32[16,3]{0,1:T(4,128)} %param.10) | copy-start | bytes 580
  7.2 49.4 %copy-start.3 = (s32[2]{0:T(128)S(1)}, s32[2]{0:T(128)}, u32[]{:S(2)}) copy-start(s32[2]{0:T(128)} %param.8) | copy-start | bytes 28
  7.2 46.2 %all-gather.9.cloned.1.call-start = ((), (), s32[]{:S(2)}) async-start(), calls=%async_computation.2 | async-start | bytes 1769472 | tf_op jit(solution)/shard_map/all_gather | solution.py:19
  13.8 111.9 %all-gather.11.cloned.1.call-start = ((), (), s32[]{:S(2)}) async-start(), calls=%async_computation.3 | async-start | bytes 7864320 | tf_op jit(solution)/shard_map/all_gather | solution.py:19
  53.4 141.3 %all-gather.7.cloned.1.call-start = ((), (), s32[]{:S(2)}) async-start(), calls=%async_computation.1 | async-start | bytes 10485760 | tf_op jit(solution)/shard_map/all_gather | solution.py:61
  207.7 8.2 %all-to-all-start = ((f32[4,2,1024]{2,1,0:T(2,128)}), f32[4,2,1024]{2,1,0:T(2,128)S(1)}, u32[]{:S(2)}, u32[]{:S(2)}) async-start(f32[4,2,1024]{2,1,0:T(2,128)} %broadcast_in_dim.15), calls=%async_computation | async-start | bytes 65536 | tf_op jit(solution)/shard_map/all_to_all | solution.py:32
Sparse Core Ops, SparseCore 0:
  13.9 39.4 all-gather.8
  55.2 70.4 all-gather.10
  127.5 67.1 all-gather.6
where the time goes:
time: 223 us
  waiting for transfers between devices  166 us (74%)
  local copies, waits for them, and re-layouts  18.7 us (8%)
  between operations  13.8 us (6%)
  matrix products  12.5 us (6%)
  blocking collectives  6.49 us (3%)
  starting transfers between devices  3.61 us (2%)
  other arithmetic  2.3 us (1%)
    all_gather x2, waiting for transfers between devices, all_blocks(): tiles = lax.all_gather(tiles, axes[k])  108 us
    all_gather x1, waiting for transfers between devices, local(): lax.all_gather(orbitals, 'orb', axis=3, tiled=True)  54.4 us
    dot_general x1, matrix products, rotate(): jnp.einsum('glpi,glmij->gmpj', values, tile_set, preferred_element_type=j...  9.84 us
    all_gather x1, blocking collectives, all_blocks(): tiles = lax.all_gather(tiles, axes[k])  6.49 us
    gather x1, local copies, waits for them, and re-layouts, select_tiles(): picked = band_full[source, column]  5.83 us
    reshape x1, local copies, waits for them, and re-layouts, laid_out(): return jnp.moveaxis(tiles, 0, dim).reshape(shape)  4.87 us
  transfers between devices with their start and end apart: 4, of which 4 were waited for; matrix products, arithmetic and copies ran while one was open for 9% of the time, Pallas kernels for 0%

commit v1 on v0

v1 whole, which is shorter than its diff:
```python
import heapq

import jax
import jax.numpy as jnp
from jax import lax
from jax.experimental import pallas as pl
from jax.experimental.pallas import tpu as pltpu
from jax.sharding import PartitionSpec as P

MESH = pl.DeviceIdType.MESH
NX, NY, NZ = 4, 4, 8
TILES = 46
A_TILES = 19
CHUNKS = 8
ROWS = 256
HALF = 128
B_SETS = {1: (0, 1, -2, 3), -1: (-1, 2, -3, 4)}


def messages():
    tile = 8 * 128 * 2
    a, b = A_TILES * tile, (TILES - A_TILES) * tile
    out = {}
    out["swap",] = ("xs", a + b, [("tiles",)])
    mine = [("swap",), ("tiles",)]
    for n in range(1, 5):
        for s in (1, -1):
            out["Bz", s, n] = (("z", s), 2 * b if n < 4 else b, mine if n == 1 else [("Bz", s, n - 1)])
    for s in (1, -1):
        out["Ay1", s] = (("y", s), 2 * a, mine)
        out["Ay2", s] = (("y", s), a, [("Ay1", s)])
    have_a = {0: mine, -1: [("Ay1", 1)], 1: [("Ay1", -1)], 2: [("Ay2", 1), ("Ay2", -1)]}
    for dy in (0, -1, 1, 2):
        for n in range(1, 5):
            for s in (1, -1):
                out["Az", s, dy, n] = (("z", s), 2 * a if n < 4 else a, have_a[dy] if n == 1 else [("Az", s, dy, n - 1)])
    have_b = {0: mine, 4: [("Bz", 1, 4), ("Bz", -1, 4)]}
    for n in range(1, 4):
        have_b[-n], have_b[n] = [("Bz", 1, n)], [("Bz", -1, n)]
    for dz in (0, -1, 1, -2, 2, -3, 3, 4):
        for s in (1, -1):
            out["By1", s, dz] = (("y", s), 2 * b, have_b[dz])
            if dz in B_SETS[s]:
                out["By2", s, dz] = (("y", s), 2 * b, [("By1", s, dz)])
    piece = 4 * HALF * 128 * 2
    for k in range(CHUNKS):
        for s in (1, -1):
            out["X1", s, k] = (("x", s), piece, [("own", k)])
    for k in range(CHUNKS):
        for s in (1, -1):
            out["X2", s, k] = (("x", s), piece, [("X1", s, k)])
            out["Xd", s, k] = ("d", piece, [("X2", s, k)])
        out["Od", k] = ("d", 2 * piece, [("own", k)])
    return out


def is_tile(key):
    return key[0] in ("swap", "Bz", "Ay1", "Ay2", "Az", "By1", "By2")


def plan():
    todo = messages()
    rate = {"xs": 46.6e3, "d": 330e3}
    free, here, due, order = {}, set(), [], []
    now = 0.0
    pending = dict(todo)

    def send_ready():
        for key in [k for k, v in pending.items() if all(need in here for need in v[2])]:
            link, size, _ = pending.pop(key)
            links = [("x", 1), ("x", -1)] if link == "xs" else [link]
            start = max([now] + [free.get(one, 0.0) for one in links])
            end = start + size / rate.get(link, 46.6e3)
            for one in links:
                free[one] = end
            heapq.heappush(due, (end + (1.1 if link == "d" else 1.9), len(order), key))
            order.append(("send", key))

    heapq.heappush(due, (0.4, -100, ("tiles",)))
    for k in range(CHUNKS):
        heapq.heappush(due, (0.5 + 0.1 * k, k - 50, ("own", k)))
    tiles_left = {key for key in todo if is_tile(key)} | {("tiles",)}
    weights, done = False, 0
    while due or done < CHUNKS:
        if due and due[0][0] <= now:
            key = heapq.heappop(due)[2]
            order.append(("wait", key))
            here.add(key)
            tiles_left.discard(key)
            send_ready()
            continue
        k = done
        ready = weights and k < CHUNKS and all(
            need in here for need in [("own", k), ("Od", k)] + [(t, s, k) for t in ("X2", "Xd") for s in (1, -1)]
        )
        if not weights and not tiles_left:
            order.append(("weights",))
            weights = True
            now += 1.5
        elif ready:
            order.append(("product", k))
            done += 1
            now += 0.6
        else:
            now = due[0][0]
    return order, now


def kernel(ids, count, pattern, band, orbitals, occ, rotated, density, T, X, F, W, O, dens, recv, sent, local, put, dsend, drecv):
    dom, orb = lax.axis_index("dom"), lax.axis_index("orb")
    x_lo, z, y = lax.div(dom, 32), lax.rem(lax.div(dom, 4), 8), lax.rem(dom, 4)
    x_hi, core = lax.div(orb, 2), lax.rem(orb, 2)
    x = x_hi * 2 + x_lo

    def at_x(step):
        return lax.rem(x + step + NX, NX)

    def at_y(step):
        return lax.rem(y + step + NY, NY)

    def at_z(step):
        return lax.rem(z + step + NZ, NZ)

    def device(px, py, pz, pc):
        return (lax.rem(px, 2) * 32 + pz * 4 + py, lax.div(px, 2) * 2 + pc)

    def orb_of(px):
        return lax.div(px, 2) * 2 + core

    swap_x = x + 1 - 2 * x_lo
    to = {
        "xs": device(swap_x, y, z, core),
        "d": device(x, y, z, 1 - core),
        "far": device(at_x(2), y, z, core),
        "cross": device(at_x(2), y, z, 1 - core),
    }
    for s in (1, -1):
        to["x", s] = device(at_x(s), y, z, core)
        to["y", s] = device(x, at_y(s), z, core)
        to["z", s] = device(x, y, at_z(s), core)

    def part(which):
        return pl.ds(0, A_TILES) if which == "A" else pl.ds(A_TILES, TILES - A_TILES)

    def lows(s, half):
        return pl.ds(0 if s > 0 else 1, 1) if half else pl.ds(0, 2)

    def piece(k, s):
        return pl.ds(k // 4 * 4, 4), pl.ds(k % 4 * ROWS + (0 if s > 0 else HALF), HALF)

    todo = messages()
    number = {key: i for i, key in enumerate(todo)}

    def copy(key):
        kind = key[0]
        if kind == "swap":
            src = dst = T.at[z, y, x_lo]
        elif kind == "Bz":
            _, s, n = key
            src = dst = T.at[at_z(-(n - 1) * s), y, lows(s, n == 4), part("B")]
        elif kind == "Ay1":
            src = dst = T.at[z, y, lows(1, False), part("A")]
        elif kind == "Ay2":
            src = dst = T.at[z, at_y(-key[1]), lows(key[1], True), part("A")]
        elif kind == "Az":
            _, s, dy, n = key
            src = dst = T.at[at_z(-(n - 1) * s), at_y(dy), lows(s, n == 4), part("A")]
        elif kind == "By1":
            src = dst = T.at[at_z(key[2]), y, lows(1, False), part("B")]
        elif kind == "By2":
            src = dst = T.at[at_z(key[2]), at_y(-key[1]), lows(1, False), part("B")]
        elif kind == "X1":
            _, s, k = key
            slots, rows = piece(k, s)
            src, dst = X.at[orb, slots, rows], F.at[0 if s > 0 else 1, k]
        elif kind == "X2":
            _, s, k = key
            slots, rows = piece(k, s)
            src, dst = F.at[0 if s > 0 else 1, k], X.at[orb_of(at_x(-s)), slots, rows]
        elif kind == "Xd":
            _, s, k = key
            slots, rows = piece(k, s)
            src = dst = X.at[orb_of(at_x(2)), slots, rows]
        else:
            k = key[1]
            src = dst = X.at[orb, pl.ds(k // 4 * 4, 4), pl.ds(k % 4 * ROWS, ROWS)]
        i = number[key]
        return pltpu.make_async_remote_copy(
            src_ref=src, dst_ref=dst, send_sem=sent.at[i], recv_sem=recv.at[i], device_id=to[todo[key][0]], device_id_type=MESH
        )

    def load(key):
        if key[0] == "tiles":
            return pltpu.make_async_copy(band.at[pl.ds(1, TILES)], T.at[z, y, x_lo], local.at[CHUNKS])
        k = key[1]
        slots, rows = pl.ds(k // 4 * 4, 4), pl.ds(k % 4 * ROWS, ROWS)
        return pltpu.make_async_copy(orbitals.at[slots, rows], X.at[orb, slots, rows], local.at[k])

    def store(k):
        slots, rows = pl.ds(k // 4 * 4, 4), pl.ds(k % 4 * ROWS, ROWS)
        return pltpu.make_async_copy(O.at[slots, rows], rotated.at[slots, rows], put.at[k])

    def weights():
        for g in range(2):
            for pair in range(2):
                for at in range(3):
                    l = pair + at
                    for side in range(2):
                        m = pair * 2 + side
                        block = (g * 2 + pair, pl.ds(at * 512, 512), pl.ds(side * 128, 128))
                        if abs(l - m) > 1:
                            W[block] = jnp.zeros((512, 128), jnp.bfloat16)
                            continue
                        source, target = ids[g, l], ids[g, m]
                        column = target - source + 1
                        inside = (column >= 0) & (column < 3)
                        column = jnp.clip(column, 0, 2)
                        last = max(l, m)
                        keep = inside & (pattern[source, column] == 1) & (last < count[g])
                        t = jnp.clip(source * 3 + column - 1, 0, TILES - 1)
                        scale = jnp.where(keep, jnp.float32(1), jnp.float32(0))
                        for low in range(2):
                            rows = T[:, :, low, t].astype(jnp.float32).reshape(256, 128) * scale
                            W[g * 2 + pair, pl.ds(at * 512 + low * 256, 256), pl.ds(side * 128, 128)] = rows.astype(jnp.bfloat16)

    def product(k):
        g, base = k // 4, k % 4 * ROWS
        rows = pl.ds(base, ROWS)
        total = jnp.zeros((ROWS, 128), jnp.float32)
        for pair in range(2):
            values = jnp.concatenate([X[q, g * 4 + pair + at, rows] for at in range(3) for q in range(4)], axis=1)
            out = jnp.dot(values, W[g * 2 + pair], preferred_element_type=jnp.float32).astype(jnp.bfloat16)
            for side in range(2):
                m = pair * 2 + side
                one = out[:, side * 128 : side * 128 + 128]
                O[g * 4 + m, rows] = one
                wide = one.astype(jnp.float32)
                total = total + wide * wide * occ[pl.ds(ids[g, m], 1), :]
        summed = lax.dot_general(
            jnp.ones((8, 128), jnp.float32), total, (((1,), (1,)), ((), ())),
            precision=lax.Precision.HIGHEST, preferred_element_type=jnp.float32,
        )
        dens[orb, pl.ds(g, 1), rows] = summed[0:1]
        store(k).start()

    load(("tiles",)).start()
    for k in range(CHUNKS):
        load(("own", k)).start()
    barrier = pltpu.get_barrier_semaphore()
    for peer in to:
        if peer != "xs":
            pl.semaphore_signal(barrier, inc=1, device_id=to[peer], device_id_type=MESH)
    pl.semaphore_wait(barrier, len(to) - 1)

    for step in plan()[0]:
        if step[0] == "send":
            copy(step[1]).start()
        elif step[0] == "wait":
            if step[1][0] in ("tiles", "own"):
                load(step[1]).wait()
            else:
                copy(step[1]).wait_recv()
        elif step[0] == "weights":
            weights()
        else:
            product(step[1])

    for key in todo:
        copy(key).wait_send()
    shares = [
        pltpu.make_async_remote_copy(
            src_ref=dens.at[orb], dst_ref=dens.at[orb], send_sem=dsend.at[i], recv_sem=drecv.at[i], device_id=to[peer], device_id_type=MESH
        )
        for i, peer in enumerate(("d", "far", "cross"))
    ]
    for share in shares:
        share.start()
    for k in range(CHUNKS):
        store(k).wait()
    for share in shares:
        share.wait_recv()
    density[...] = dens[0] + dens[1] + dens[2] + dens[3]
    for share in shares:
        share.wait_send()


def local(orbitals, slot_ids, slot_count, band_tiles, pattern, occupation):
    smem, hbm, vmem = (pl.BlockSpec(memory_space=s) for s in (pltpu.SMEM, pl.ANY, pltpu.VMEM))
    n = len(messages())
    rotated, density = pl.pallas_call(
        kernel,
        out_shape=(jax.ShapeDtypeStruct((8, 1024, 128), jnp.bfloat16), jax.ShapeDtypeStruct((2, 1024), jnp.float32)),
        in_specs=[smem, smem, smem, hbm, hbm, vmem],
        out_specs=(hbm, vmem),
        scratch_shapes=[
            pltpu.VMEM((NZ, NY, 2, TILES, 8, 128), jnp.bfloat16),
            pltpu.VMEM((4, 8, 1024, 128), jnp.bfloat16),
            pltpu.VMEM((2, CHUNKS, 4, HALF, 128), jnp.bfloat16),
            pltpu.VMEM((4, 1536, 256), jnp.bfloat16),
            pltpu.VMEM((8, 1024, 128), jnp.bfloat16),
            pltpu.VMEM((4, 2, 1024), jnp.float32),
            pltpu.SemaphoreType.DMA((n,)),
            pltpu.SemaphoreType.DMA((n,)),
            pltpu.SemaphoreType.DMA((CHUNKS + 1,)),
            pltpu.SemaphoreType.DMA((CHUNKS,)),
            pltpu.SemaphoreType.DMA((3,)),
            pltpu.SemaphoreType.DMA((3,)),
        ],
        compiler_params=pltpu.CompilerParams(collective_id=0, has_side_effects=True, vmem_limit_bytes=48 * 1024 * 1024),
    )(slot_ids, slot_count, pattern, band_tiles.reshape(48, 8, 128), orbitals.reshape(8, 1024, 128), occupation)
    return rotated.reshape(2, 4, 1024, 128), density


def solution(mesh):
    return jax.shard_map(
        local,
        mesh=mesh,
        in_specs=(
            P("dom", None, None, "orb"),
            P("dom", None),
            P("dom"),
            P(None, None, "dom", "orb"),
            P(),
            P(None, "orb"),
        ),
        out_specs=(P("dom", None, None, "orb"), P("dom", None)),
        check_vma=False,
    )
```

time: 223 us -> 76.5 us (0.34)
  waiting for transfers between devices: 166 us -> 0 us
  Pallas kernels: 0 us -> 68.5 us
  between operations: 13.8 us -> 0.64 us
  matrix products: 12.5 us -> 0 us
  local copies, waits for them, and re-layouts: 18.7 us -> 7.19 us
  blocking collectives: 6.49 us -> 0 us
  starting transfers between devices: 3.61 us -> 0 us
  other arithmetic: 2.3 us -> 0 us
    all_gather x3 -> x0, waiting for transfers between devices: 163 us -> none  [the longest x2 108 us: all_blocks(): tiles = lax.all_gather(tiles, axes[k])]
    pallas_call x0 -> x1, Pallas kernels: none -> 68.5 us  [local(): pl.pallas_call(kernel, out_shape=(jax.ShapeDtypeStruct((8, 1024, 128), jn...]
    dot_general x3 -> x0, matrix products: 12.5 us -> none  [the longest x1 9.84 us: rotate(): jnp.einsum('glpi,glmij->gmpj', values, tile_set, preferred_element_type=j...]
    gather x2 -> x0, local copies, waits for them, and re-layouts: 6.59 us -> none  [the longest x1 5.83 us: select_tiles(): picked = band_full[source, column]]
    all_gather x1 -> x0, blocking collectives: 6.49 us -> none  [all_blocks(): tiles = lax.all_gather(tiles, axes[k])]
    reshape x1 -> x0, local copies, waits for them, and re-layouts: 4.87 us -> none  [laid_out(): return jnp.moveaxis(tiles, 0, dim).reshape(shape)]
    unnamed x9 -> x13, local copies, waits for them, and re-layouts: 2.56 us -> 7.19 us
    transpose x1 -> x0, local copies, waits for them, and re-layouts: 3.89 us -> none  [all_blocks(): tiles = tiles.transpose(*back, *range(len(axes), tiles.ndim))]
  transfers between devices with their start and end apart: 4 -> 0, of which waited for: 4 -> 0; matrix products, arithmetic and copies ran while one was open for 9% -> 0% of each run, Pallas kernels for 0% -> 0%
where the time goes in v1:
time: 76.5 us; the launch traced here: 76.3 us
  Pallas kernels  68.5 us (90%)
  local copies, waits for them, and re-layouts  7.19 us (9%)
    pallas_call x1, Pallas kernels, local(): pl.pallas_call(kernel, out_shape=(jax.ShapeDtypeStruct((8, 1024, 128), jn...  68.5 us
    unnamed x13, local copies, waits for them, and re-layouts  7.19 us

profile of v1, /device:TPU:1, one launch (start us, length us, event | category | flops | bytes accessed | tf_op | source)
XLA Modules:
  0.0 76.3 jit_solution(8089409381325944368)
XLA Ops:
  0.6 0.8 copy.8.pattern
  1.4 0.0 copy-start
  1.4 1.6 %copy-done = bf16[2,4,1024,128]{3,2,1,0:T(8,128)(2,1)S(1)} copy-done((bf16[2,4,1024,128]{3,2,1,0:T(8,128)(2,1)S(1)}, bf16[2,4,1024,128]{3,2,1,0:T(8,128)(2,1)}, u32[]{:S(2)}) %copy-start) | copy-done | bytes 2097176
  3.0 0.0 copy-start.1
  3.0 0.9 %copy-done.1 = bf16[16,3,8,128]{3,2,1,0:T(8,128)(2,1)S(1)} copy-done((bf16[16,3,8,128]{3,2,1,0:T(8,128)(2,1)S(1)}, bf16[16,3,8,128]{3,2,1,0:T(8,128)(2,1)}, u32[]{:S(2)}) %copy-start.1) | copy-done | bytes 98328
  3.9 0.0 copy-start.2
  3.9 0.7 copy-done.2
  4.6 0.0 copy-start.3
  4.6 0.7 copy-done.3
  5.2 0.0 copy-start.4
  5.3 0.7 copy-done.4
  5.9 68.5 %shard_map.77 = (bf16[8,1024,128]{2,1,0:T(8,128)(2,1)S(1)}, f32[2,1024]{1,0:T(2,128)S(1)}) custom-call(s32[2,4]{1,0:T(2,128)S(1)} %copy-done.3, s32[2]{0:T(128)S(1)} %copy-done.4, s32[16,3]{1,0:T(8,128)S(1)} %copy.8.pattern, bf16[48,8,128]{2,1,0:T(8,128)(2,1)S(1)} %bitcast.5, bf16[8,1024,128]{2,1,0:T(8,128)(2,1)S(1)} %bitcast.3, f32[16,128]{1,0:T(8,128)S(1)} %copy-done.2), custom_call_target="tpu_custom_call" | custom-call | tf_op jit(solution)/shard_map/pallas_call | solution.py:290
  74.4 1.3 %copy.11 = bf16[2,4,1024,128]{3,2,1,0:T(8,128)(2,1)} copy(bf16[2,4,1024,128]{3,2,1,0:T(8,128)(2,1)S(1)} %bitcast.4) | data formatting | bytes 4194304
  75.7 0.6 copy.12
Async XLA Ops:
  1.4 1.6 %copy-start = (bf16[2,4,1024,128]{3,2,1,0:T(8,128)(2,1)S(1)}, bf16[2,4,1024,128]{3,2,1,0:T(8,128)(2,1)}, u32[]{:S(2)}) copy-start(bf16[2,4,1024,128]{3,2,1,0:T(8,128)(2,1)} %param.6) | copy-start | bytes 6291460
  3.0 0.9 %copy-start.1 = (bf16[16,3,8,128]{3,2,1,0:T(8,128)(2,1)S(1)}, bf16[16,3,8,128]{3,2,1,0:T(8,128)(2,1)}, u32[]{:S(2)}) copy-start(bf16[16,3,8,128]{3,2,1,0:T(8,128)(2,1)} %param.9) | copy-start | bytes 294916
  3.9 0.7 copy-start.2
  4.6 0.7 copy-start.3
  5.2 0.7 copy-start.4

commit v2 on v1

v2 whole, which is shorter than its diff:
```python
import functools
import heapq

import jax
import jax.numpy as jnp
from jax import lax
from jax.experimental import pallas as pl
from jax.experimental.pallas import tpu as pltpu
from jax.sharding import PartitionSpec as P

MESH = pl.DeviceIdType.MESH
NX, NY, NZ = 4, 4, 8
TILES = 46
A_TILES = 18
VMEM_BYTES = 67043328 - 2097152 - 8192
B_SETS = {1: (0, 1, -2, 3), -1: (-1, 2, -3, 4)}
CHUNKS = [(0, a, 128) for a in range(0, 512, 128)] + [(1, 0, 128), (1, 128, 128), (1, 256, 128), (1, 384, 64), (1, 448, 32), (1, 480, 32)]
UNITS = [(0, 0, 256), (0, 256, 256), (1, 0, 256), (1, 256, 128), (1, 384, 64), (1, 448, 32), (1, 480, 32)]
TAIL = 384
DEPTH = 2


def messages():
    tile = 8 * 128 * 2
    a, b = A_TILES * tile, (TILES - A_TILES) * tile
    out = {}

    def add(key, link, size, needs, group=None):
        out[key] = (link, size, needs, group or key)

    add(("swap",), "xs", a + b, [("tiles",)])
    mine = [("swap",), ("z",)]
    for n in range(1, 5):
        for s in (1, -1):
            add(("Bz", s, n), ("z", s), 2 * b if n < 4 else b, mine if n == 1 else [("Bz", s, n - 1)], ("Bz4",) if n == 4 else None)
    for s in (1, -1):
        add(("Ay1", s), ("y", s), 2 * a, mine)
        add(("Ay2", s), ("y", s), a, [("Ay1", s)], ("Ay2",))
    have_a = {0: mine, -1: [("Ay1", 1)], 1: [("Ay1", -1)], 2: [("Ay2",)]}
    for dy in (0, -1, 1, 2):
        for n in range(1, 5):
            for s in (1, -1):
                needs = have_a[dy] if n == 1 else [("Az", s, dy, n - 1)]
                add(("Az", s, dy, n), ("z", s), 2 * a if n < 4 else a, needs, ("Az4",) if n == 4 else None)
    have_b = {0: mine, 4: [("Bz4",)]}
    for n in range(1, 4):
        have_b[-n], have_b[n] = [("Bz", 1, n)], [("Bz", -1, n)]
    for dz in (0, -1, 1, -2, 2, -3, 3, 4):
        for s in (1, -1):
            onward = dz in B_SETS[s]
            add(("By1", s, dz), ("y", s), 2 * b, have_b[dz], None if onward else ("By1", s))
            if onward:
                add(("By2", s, dz), ("y", s), 2 * b, [("By1", s, dz)], ("By2",))
    row = 4 * 128 * 2
    for i in range(4):
        for s in (1, -1):
            add(("X1", s, i), ("x", s), 256 * row, [("own", i // 2)])
    for g in range(2):
        add(("Od", g), "d", 1024 * row, [("own", g)])
    for k, (g, first, rows) in enumerate(CHUNKS):
        for s in (1, -1):
            add(("X2", s, k), ("x", s), rows * row, [("X1", s, g * 2 + first // 256)], ("X2", k))
        add(("Xd", k), "d", 2 * rows * row, [("X2", k)])
    return out


def plan():
    todo = messages()
    rate = {"d": 690e3}
    left, after = {}, {}
    for key, (_, _, needs, group) in todo.items():
        left.setdefault(group, set()).add(key)
        for need in needs:
            after.setdefault(need, []).append(key)

    @functools.lru_cache(None)
    def path(key):
        link, size, _, group = todo[key]
        return size / rate.get(link, 45e3) + 1.9 + max([path(k) for k in after.get(group, [])], default=0)

    free, here, due, order, pending = {}, set(), [], [], dict(todo)
    now = 0.0

    def send_ready():
        ready = [k for k, v in pending.items() if all(need in here for need in v[2])]
        for key in sorted(ready, key=lambda k: -path(k) if k[0][0] in "AB" else 0):
            link, size, _, group = todo[key]
            busy = [t for t in free.get(link, []) if t > now]
            if link[0] in "yz" and len(busy) >= DEPTH:
                continue
            pending.pop(key)
            links = [("x", 1), ("x", -1)] if link == "xs" else [link]
            start = max([now] + [t for one in links for t in free.get(one, [])[-1:]])
            end = start + size / rate.get(link, 45e3)
            for one in links:
                free.setdefault(one, []).append(end)
            heapq.heappush(due, (end + (1.0 if link == "d" else 1.9), len(order), key))
            order.append(("send", key))

    for i, group in enumerate([("tiles",), ("own", 0), ("own", 1), ("z",)]):
        heapq.heappush(due, (0.01 * i, i - 50, group))
        left[group] = {group}
    tiles_left = {g for g in left if g[0] in ("tiles", "swap", "Bz", "Bz4", "Ay1", "Ay2", "Az", "Az4", "By1", "By2")}
    weights, done = False, 0
    while due or done < len(UNITS):
        if due and due[0][0] <= now:
            key = heapq.heappop(due)[2]
            group = todo[key][3] if key in todo else key
            left[group].discard(key)
            if not left[group]:
                order.append(("wait", group))
                here.add(group)
                tiles_left.discard(group)
            send_ready()
            continue
        ready = False
        if weights and done < len(UNITS):
            g, first, rows = UNITS[done]
            parts = [k for k, (cg, ca, _) in enumerate(CHUNKS) if cg == g and first <= ca < first + rows]
            ready = ("Od", g) in here and all((t, k) in here for t in ("X2", "Xd") for k in parts)
        if not weights and not tiles_left:
            order.append(("weights",))
            weights = True
            now += 0.7
        elif ready:
            order.append(("product", done))
            now += 0.4 + 0.4 * UNITS[done][2] / 128
            done += 1
        else:
            now = due[0][0]
    assert not pending
    return order, now


def kernel(
    ids_in, count_in, pattern_in, band, orbitals, occ_in, rotated, density,
    ids, count, pattern, occ, T, X, F, W, D, dens, recv, sent, local, small, shared, ready,
):
    dom, orb = lax.axis_index("dom"), lax.axis_index("orb")
    x_lo, z, y = lax.div(dom, 32), lax.rem(lax.div(dom, 4), 8), lax.rem(dom, 4)
    x_hi, core = lax.div(orb, 2), lax.rem(orb, 2)
    x = x_hi * 2 + x_lo

    def at_x(step):
        return lax.rem(x + step + NX, NX)

    def at_y(step):
        return lax.rem(y + step + NY, NY)

    def at_z(step):
        return lax.rem(z + step + NZ, NZ)

    def device(px, py, pz, pc):
        return (lax.rem(px, 2) * 32 + pz * 4 + py, lax.div(px, 2) * 2 + pc)

    far = lax.div(at_x(2), 2) * 2 + core
    to = {"xs": device(x + 1 - 2 * x_lo, y, z, core), "d": device(x, y, z, 1 - core)}
    for s in (1, -1):
        to["x", s] = device(at_x(s), y, z, core)
        to["y", s] = device(x, at_y(s), z, core)
        to["z", s] = device(x, y, at_z(s), core)

    A, B, BOTH, ALL = pl.ds(0, A_TILES), pl.ds(A_TILES, TILES - A_TILES), pl.ds(0, 2), slice(None)

    def lows(s, half):
        return pl.ds(0 if s > 0 else 1, 1) if half else BOTH

    def side(s):
        return 0 if s > 0 else 1

    todo = messages()
    groups = list(dict.fromkeys(v[3] for v in todo.values()))
    number = {group: i for i, group in enumerate(groups)}

    def ends(key):
        kind = key[0]
        if kind == "swap":
            return (T.at[z, y, x_lo],) * 2
        if kind == "Bz":
            _, s, n = key
            return (T.at[at_z(-(n - 1) * s), y, lows(s, n == 4), B],) * 2
        if kind == "Ay1":
            return (T.at[z, y, BOTH, A],) * 2
        if kind == "Ay2":
            return (T.at[z, at_y(-key[1]), lows(key[1], True), A],) * 2
        if kind == "Az":
            _, s, dy, n = key
            return (T.at[at_z(-(n - 1) * s), at_y(dy), lows(s, n == 4), A],) * 2
        if kind == "By1":
            return (T.at[at_z(key[2]), y, BOTH, B],) * 2
        if kind == "By2":
            return (T.at[at_z(key[2]), at_y(-key[1]), BOTH, B],) * 2
        if kind == "X1":
            _, s, i = key
            rows = pl.ds(i % 2 * 256, 256)
            return X.at[orb, i // 2, ALL, side(s), rows], F.at[side(s), i // 2, ALL, rows]
        if kind == "X2":
            _, s, k = key
            g, first, rows = CHUNKS[k]
            source = lax.div(at_x(-s), 2) * 2 + core
            return F.at[side(s), g, ALL, pl.ds(first, rows)], X.at[source, g, ALL, side(s), pl.ds(first, rows)]
        if kind == "Xd":
            g, first, rows = CHUNKS[key[1]]
            return (X.at[far, g, ALL, ALL, pl.ds(first, rows)],) * 2
        return (X.at[orb, key[1]],) * 2

    def copy(key):
        src, dst = ends(key)
        return pltpu.make_async_remote_copy(
            src_ref=src, dst_ref=dst, send_sem=sent.at[0], recv_sem=recv.at[number[todo[key][3]]],
            device_id=to[todo[key][0]], device_id_type=MESH,
        )

    def landed(group):
        kind = group[0]
        if kind == "Bz4":
            where = T.at[z, y, BOTH, B]
        elif kind == "Ay2":
            where = T.at[z, y, BOTH, A]
        elif kind == "Az4":
            where = T.at[z, ALL, BOTH, A]
        elif kind == "By1" and len(group) == 2:
            where = T.at[pl.ds(0, 4), y, BOTH, B]
        elif kind == "By2":
            where = T.at[ALL, y, BOTH, B]
        elif kind == "X2":
            g, first, rows = CHUNKS[group[1]]
            where = X.at[far, g, ALL, ALL, pl.ds(first, rows)]
        else:
            where = ends(group)[1]
        pltpu.make_async_copy(where, where, recv.at[number[group]]).wait()

    loads = {("tiles",): pltpu.make_async_copy(band.at[pl.ds(1, TILES)], T.at[z, y, x_lo], local.at[0])}
    for g in range(2):
        loads["own", g] = pltpu.make_async_copy(orbitals.at[g], X.at[orb, g], local.at[1 + g])
    tables = [
        pltpu.make_async_copy(here, there, small.at[i])
        for i, (here, there) in enumerate(((ids_in, ids), (count_in, count), (pattern_in, pattern), (occ_in, occ)))
    ]

    def weights():
        for g in range(2):
            for pair in range(2):
                for at in range(3):
                    l = pair + at
                    for half in range(2):
                        m = pair * 2 + half
                        columns = pl.ds(half * 128, 128)
                        if abs(l - m) > 1:
                            W[g * 2 + pair, pl.ds(at * 512, 512), columns] = jnp.zeros((512, 128), jnp.bfloat16)
                            continue
                        source, target = ids[g, l], ids[g, m]
                        column = target - source + 1
                        inside = (column >= 0) & (column < 3)
                        column = jnp.clip(column, 0, 2)
                        keep = inside & (pattern[column, source] == 1) & (max(l, m) < count[g])
                        t = jnp.clip(source * 3 + column - 1, 0, TILES - 1)
                        scale = jnp.where(keep, jnp.float32(1), jnp.float32(0))
                        for low in range(2):
                            rows = T[:, :, low, t].astype(jnp.float32).reshape(256, 128) * scale
                            W[g * 2 + pair, pl.ds(at * 512 + low * 256, 256), columns] = rows.astype(jnp.bfloat16)

    def lane_sums(total):
        high = total.astype(jnp.bfloat16)
        rest = total - high.astype(jnp.float32)
        middle = rest.astype(jnp.bfloat16)
        low = (rest - middle.astype(jnp.float32)).astype(jnp.bfloat16)
        return lax.dot_general(
            jnp.ones((8, 384), jnp.bfloat16), jnp.concatenate([high, middle, low], axis=1),
            (((1,), (1,)), ((), ())), preferred_element_type=jnp.float32,
        )

    def product(u):
        g, first, n = UNITS[u]
        rows = pl.ds(first, n)
        total = jnp.zeros((2 * n, 128), jnp.float32)
        for pair in range(2):
            values = jnp.concatenate(
                [
                    jnp.concatenate([X[q, g, pair + at, half, rows] for at in range(3) for q in range(4)], axis=1)
                    for half in range(2)
                ],
                axis=0,
            )
            out = jnp.dot(values, W[g * 2 + pair], preferred_element_type=jnp.float32).astype(jnp.bfloat16)
            for which in range(2):
                m = pair * 2 + which
                one = out[:, which * 128 : which * 128 + 128]
                for half in range(2):
                    rotated[g, m, half, rows] = one[half * n : half * n + n]
                wide = one.astype(jnp.float32)
                total = total + wide * wide * occ[pl.ds(ids[g, m], 1), :]
        tail = g == 1 and first >= TAIL
        if tail:
            for half in range(2):
                D[half, pl.ds(first - TAIL, n)] = total[half * n : half * n + n]
            if u < len(UNITS) - 1:
                return
            first, n = TAIL, 512 - TAIL
            total = D[...].reshape(2 * n, 128)
        summed = lane_sums(total)
        for half in range(2):
            dens[orb, pl.ds(g, 1), pl.ds(half * 512 + first, n)] = summed[0:1, half * n : half * n + n]

    for load in loads.values():
        load.start()
    for table in tables:
        table.start()

    barrier = pltpu.get_barrier_semaphore()
    for step in (1, -1, 2):
        pl.semaphore_signal(barrier, inc=1, device_id=device(at_x(step), y, z, 0), device_id_type=MESH)
    for step in (1, -1):
        pl.semaphore_signal(barrier, inc=1, device_id=device(x, at_y(step), z, 1), device_id_type=MESH)
        pl.semaphore_signal(barrier, inc=1, device_id=device(x, y, at_z(step), 1), device_id_type=MESH)

    @pl.when(core == 1)
    def _():
        pl.semaphore_signal(barrier, inc=1, device_id=device(x, y, z, 0), device_id_type=MESH)

    @pl.when(core == 0)
    def _():
        pl.semaphore_wait(barrier, 7)
        pl.semaphore_signal(ready, inc=1, device_id=device(x, y, z, 1), device_id_type=MESH)

    @pl.when(core == 1)
    def _():
        pl.semaphore_wait(ready, 1)

    def neighbours():
        @pl.when(core == 1)
        def _():
            pl.semaphore_wait(barrier, 8)
            pl.semaphore_signal(ready, inc=1, device_id=device(x, y, z, 0), device_id_type=MESH)

        @pl.when(core == 0)
        def _():
            pl.semaphore_wait(ready, 1)

    for step in plan()[0]:
        if step[0] == "send":
            copy(step[1]).start()
        elif step[0] == "product":
            product(step[1])
        elif step[0] == "weights":
            for table in tables:
                table.wait()
            weights()
        elif step[1] in loads:
            loads[step[1]].wait()
        elif step[1] == ("z",):
            neighbours()
        else:
            landed(step[1])

    for key in todo:
        copy(key).wait_send()
    shares = [
        pltpu.make_async_remote_copy(
            src_ref=dens.at[orb], dst_ref=dens.at[orb], send_sem=shared.at[0], recv_sem=shared.at[1], device_id=peer, device_id_type=MESH
        )
        for peer in (device(at_x(2), y, z, core), device(at_x(2), y, z, 1 - core), to["d"])
    ]
    for share in shares:
        share.start()
    three = dens.at[pl.ds(0, 3)]
    pltpu.make_async_copy(three, three, shared.at[1]).wait()
    density[...] = dens[0] + dens[1] + dens[2] + dens[3]
    pltpu.make_async_copy(three, three, shared.at[0]).wait()


def write_out(held, held_density, rotated, density, sem):
    copies = [pltpu.make_async_copy(held.at[g, m], rotated.at[g, m], sem.at[g * 4 + m]) for g in range(2) for m in range(4)]
    copies.append(pltpu.make_async_copy(held_density, density, sem.at[8]))
    for one in copies:
        one.start()
    for one in copies:
        one.wait()


def local(orbitals, slot_ids, slot_count, band_tiles, pattern, occupation):
    hbm, anywhere = (pl.BlockSpec(memory_space=s) for s in (pltpu.HBM, pl.ANY))
    n = len({v[3] for v in messages().values()})
    values, sums = ((2, 4, 2, 512, 128), jnp.bfloat16), ((2, 1024), jnp.float32)
    held = pl.pallas_call(
        kernel,
        out_shape=(pltpu.VMEM(*values), pltpu.VMEM(*sums)),
        in_specs=[hbm] * 6,
        scratch_shapes=[
            pltpu.SMEM((2, 4), jnp.int32),
            pltpu.SMEM((2,), jnp.int32),
            pltpu.SMEM((3, 16), jnp.int32),
            pltpu.VMEM((16, 128), jnp.float32),
            pltpu.VMEM((NZ, NY, 2, TILES, 8, 128), jnp.bfloat16),
            pltpu.VMEM((4, 2, 4, 2, 512, 128), jnp.bfloat16),
            pltpu.VMEM((2, 2, 4, 512, 128), jnp.bfloat16),
            pltpu.VMEM((4, 1536, 256), jnp.bfloat16),
            pltpu.VMEM((2, 512 - TAIL, 128), jnp.float32),
            pltpu.VMEM((4, 2, 1024), jnp.float32),
            pltpu.SemaphoreType.DMA((n,)),
            pltpu.SemaphoreType.DMA((1,)),
            pltpu.SemaphoreType.DMA((3,)),
            pltpu.SemaphoreType.DMA((4,)),
            pltpu.SemaphoreType.DMA((2,)),
            pltpu.SemaphoreType.REGULAR,
        ],
        compiler_params=pltpu.CompilerParams(collective_id=0, has_side_effects=True, vmem_limit_bytes=VMEM_BYTES),
    )(slot_ids, slot_count, pattern.T, band_tiles.reshape(48, 8, 128), orbitals.reshape(2, 4, 2, 512, 128), occupation)
    rotated, density = pl.pallas_call(
        write_out,
        out_shape=(jax.ShapeDtypeStruct(*values), jax.ShapeDtypeStruct(*sums)),
        in_specs=[anywhere] * 2,
        out_specs=(hbm, hbm),
        scratch_shapes=[pltpu.SemaphoreType.DMA((9,))],
        compiler_params=pltpu.CompilerParams(vmem_limit_bytes=1024 * 1024),
    )(*held)
    return rotated.reshape(2, 4, 1024, 128), density


def solution(mesh):
    return jax.shard_map(
        local,
        mesh=mesh,
        in_specs=(
            P("dom", None, None, "orb"),
            P("dom", None),
            P("dom"),
            P(None, None, "dom", "orb"),
            P(),
            P(None, "orb"),
        ),
        out_specs=(P("dom", None, None, "orb"), P("dom", None)),
        check_vma=False,
    )
```

time: 76.5 us -> 65.5 us (0.86)
  local copies, waits for them, and re-layouts: 7.19 us -> 0 us
  Pallas kernels: 68.5 us -> 64.7 us
    unnamed x13 -> x0, local copies, waits for them, and re-layouts: 7.19 us -> none
    pallas_call x1 -> x2, Pallas kernels: 68.5 us -> 64.7 us  [the longest x1 63.3 us: local(): pl.pallas_call(kernel, out_shape=(pltpu.VMEM(*values), pltpu.VMEM(*sums))...]
where the time goes in v2:
time: 65.5 us; the launch traced here: 65.4 us
  Pallas kernels  64.7 us (99%)
    pallas_call x1, Pallas kernels, local(): pl.pallas_call(kernel, out_shape=(pltpu.VMEM(*values), pltpu.VMEM(*sums))...  63.3 us
    pallas_call x1, Pallas kernels, local(): pl.pallas_call(write_out, out_shape=(jax.ShapeDtypeStruct(*values), jax.S...  1.39 us

profile of v2, /device:TPU:1, one launch (start us, length us, event | category | flops | bytes accessed | tf_op | source)
XLA Modules:
  0.0 65.4 jit_solution(5493294108953291030)
XLA Ops:
  0.6 63.3 %shard_map.77 = (bf16[2,4,2,512,128]{4,3,2,1,0:T(8,128)(2,1)S(1)}, f32[2,1024]{1,0:T(2,128)S(1)}) custom-call(s32[2,4]{1,0:T(2,128)} %ids_in.1, s32[2]{0:T(128)} %count_in.1, s32[3,16]{1,0:T(4,128)} %bitcast.6, bf16[48,8,128]{2,1,0:T(8,128)(2,1)} %bitcast.5, bf16[2,4,2,512,128]{4,3,2,1,0:T(8,128)(2,1)} %bitcast.4, f32[16,128]{1,0:T(8,128)} %occ_in.1), custom_call_target="tpu_custom_call" | custom-call | tf_op jit(solution)/shard_map/pallas_call | solution.py:385
  64.0 1.4 %shard_map.78 = (bf16[2,4,2,512,128]{4,3,2,1,0:T(8,128)(2,1)}, f32[2,1024]{1,0:T(2,128)}) custom-call(bf16[2,4,2,512,128]{4,3,2,1,0:T(8,128)(2,1)S(1)} %get-tuple-element.6.held, f32[2,1024]{1,0:T(2,128)S(1)} %get-tuple-element.7.held_density), custom_call_target="tpu_custom_call" | custom-call | tf_op jit(solution)/shard_map/pallas_call | solution.py:409

commit v3 on v2

--- a/solution.py
+++ b/solution.py
@@ -14,7 +14,7 @@
 A_TILES = 18
 VMEM_BYTES = 67043328 - 2097152 - 8192
 B_SETS = {1: (0, 1, -2, 3), -1: (-1, 2, -3, 4)}
-CHUNKS = [(0, a, 128) for a in range(0, 512, 128)] + [(1, 0, 128), (1, 128, 128), (1, 256, 128), (1, 384, 64), (1, 448, 32), (1, 480, 32)]
+CHUNKS = [(0, 0, 256), (0, 256, 256), (1, 0, 128), (1, 128, 128), (1, 256, 128), (1, 384, 64), (1, 448, 32), (1, 480, 32)]
 UNITS = [(0, 0, 256), (0, 256, 256), (1, 0, 256), (1, 256, 128), (1, 384, 64), (1, 448, 32), (1, 480, 32)]
 TAIL = 384
 DEPTH = 2
@@ -34,9 +34,9 @@
         for s in (1, -1):
             add(("Bz", s, n), ("z", s), 2 * b if n < 4 else b, mine if n == 1 else [("Bz", s, n - 1)], ("Bz4",) if n == 4 else None)
     for s in (1, -1):
-        add(("Ay1", s), ("y", s), 2 * a, mine)
-        add(("Ay2", s), ("y", s), a, [("Ay1", s)], ("Ay2",))
-    have_a = {0: mine, -1: [("Ay1", 1)], 1: [("Ay1", -1)], 2: [("Ay2",)]}
+        add(("Ay1", s), ("y", s), 2 * a, mine, ("Ay1",))
+        add(("Ay2", s), ("y", s), a, [("Ay1",)], ("Ay2",))
+    have_a = {0: mine, -1: [("Ay1",)], 1: [("Ay1",)], 2: [("Ay2",)]}
     for dy in (0, -1, 1, 2):
         for n in range(1, 5):
             for s in (1, -1):
@@ -54,14 +54,20 @@
     row = 4 * 128 * 2
     for i in range(4):
         for s in (1, -1):
-            add(("X1", s, i), ("x", s), 256 * row, [("own", i // 2)])
-    for g in range(2):
-        add(("Od", g), "d", 1024 * row, [("own", g)])
+            add(("X1", s, i), ("x", s), 256 * row, [("own", i // 2)], ("X1", i))
+    add(("Od",), "d", 2048 * row, [("own", 0), ("own", 1)])
     for k, (g, first, rows) in enumerate(CHUNKS):
         for s in (1, -1):
-            add(("X2", s, k), ("x", s), rows * row, [("X1", s, g * 2 + first // 256)], ("X2", k))
+            add(("X2", s, k), ("x", s), rows * row, [("X1", g * 2 + first // 256)], ("X2", k))
         add(("Xd", k), "d", 2 * rows * row, [("X2", k)])
     return out
+
+
+def chunks_of(u):
+    if u >= len(UNITS):
+        return []
+    g, first, rows = UNITS[u]
+    return [k for k, (cg, ca, _) in enumerate(CHUNKS) if cg == g and first <= ca < first + rows]
 
 
 def plan():
@@ -98,7 +104,7 @@
             order.append(("send", key))
 
     for i, group in enumerate([("tiles",), ("own", 0), ("own", 1), ("z",)]):
-        heapq.heappush(due, (0.01 * i, i - 50, group))
+        heapq.heappush(due, (3.0 if group == ("z",) else 0.01 * i, i - 50, group))
         left[group] = {group}
     tiles_left = {g for g in left if g[0] in ("tiles", "swap", "Bz", "Bz4", "Ay1", "Ay2", "Az", "Az4", "By1", "By2")}
     weights, done = False, 0
@@ -113,16 +119,16 @@
                 tiles_left.discard(group)
             send_ready()
             continue
-        ready = False
-        if weights and done < len(UNITS):
-            g, first, rows = UNITS[done]
-            parts = [k for k, (cg, ca, _) in enumerate(CHUNKS) if cg == g and first <= ca < first + rows]
-            ready = ("Od", g) in here and all((t, k) in here for t in ("X2", "Xd") for k in parts)
+        ready = weights and done < len(UNITS) and ("Od",) in here
+        if ready:
+            ready = all((t, k) in here for t in ("X2", "Xd") for k in chunks_of(done)) and all(("X2", k) in here for k in chunks_of(done + 1))
         if not weights and not tiles_left:
             order.append(("weights",))
             weights = True
             now += 0.7
         elif ready:
+            if UNITS[done][:2] == (1, TAIL):
+                order.append(("share",))
             order.append(("product", done))
             now += 0.4 + 0.4 * UNITS[done][2] / 128
             done += 1
@@ -134,7 +140,7 @@
 
 def kernel(
     ids_in, count_in, pattern_in, band, orbitals, occ_in, rotated, density,
-    ids, count, pattern, occ, T, X, F, W, D, dens, recv, sent, local, small, shared, ready,
+    ids, count, pattern, occ, T, X, F, W, D, dens, tails, recv, sent, local, shared, ready,
 ):
     dom, orb = lax.axis_index("dom"), lax.axis_index("orb")
     x_lo, z, y = lax.div(dom, 32), lax.rem(lax.div(dom, 4), 8), lax.rem(dom, 4)
@@ -202,7 +208,7 @@
         if kind == "Xd":
             g, first, rows = CHUNKS[key[1]]
             return (X.at[far, g, ALL, ALL, pl.ds(first, rows)],) * 2
-        return (X.at[orb, key[1]],) * 2
+        return (X.at[orb],) * 2
 
     def copy(key):
         src, dst = ends(key)
@@ -215,8 +221,12 @@
         kind = group[0]
         if kind == "Bz4":
             where = T.at[z, y, BOTH, B]
+        elif kind == "Ay1":
+            where = T.at[z, pl.ds(0, 2), BOTH, A]
         elif kind == "Ay2":
             where = T.at[z, y, BOTH, A]
+        elif kind == "X1":
+            where = F.at[ALL, group[1] // 2, ALL, pl.ds(group[1] % 2 * 256, 256)]
         elif kind == "Az4":
             where = T.at[z, ALL, BOTH, A]
         elif kind == "By1" and len(group) == 2:
@@ -234,8 +244,8 @@
     for g in range(2):
         loads["own", g] = pltpu.make_async_copy(orbitals.at[g], X.at[orb, g], local.at[1 + g])
     tables = [
-        pltpu.make_async_copy(here, there, small.at[i])
-        for i, (here, there) in enumerate(((ids_in, ids), (count_in, count), (pattern_in, pattern), (occ_in, occ)))
+        pltpu.make_async_copy(here, there, local.at[3])
+        for here, there in ((ids_in, ids), (count_in, count), (pattern_in, pattern), (occ_in, occ))
     ]
 
     def weights():
@@ -296,8 +306,11 @@
                 D[half, pl.ds(first - TAIL, n)] = total[half * n : half * n + n]
             if u < len(UNITS) - 1:
                 return
-            first, n = TAIL, 512 - TAIL
-            total = D[...].reshape(2 * n, 128)
+            n = 512 - TAIL
+            summed = lane_sums(D[...].reshape(2 * n, 128))
+            for half in range(2):
+                tails[orb, pl.ds(half, 1)] = summed[0:1, half * n : half * n + n]
+            return
         summed = lane_sums(total)
         for half in range(2):
             dens[orb, pl.ds(g, 1), pl.ds(half * 512 + first, n)] = summed[0:1, half * n : half * n + n]
@@ -337,11 +350,25 @@
         def _():
             pl.semaphore_wait(ready, 1)
 
+    def share(sums, which):
+        for peer in (device(at_x(2), y, z, core), device(at_x(2), y, z, 1 - core), to["d"]):
+            pltpu.make_async_remote_copy(
+                src_ref=sums.at[orb], dst_ref=sums.at[orb], send_sem=shared.at[2 * which], recv_sem=shared.at[2 * which + 1],
+                device_id=peer, device_id_type=MESH,
+            ).start()
+
+    def shared_by_all(sums, which):
+        for end in range(2):
+            three = sums.at[pl.ds(0, 3)]
+            pltpu.make_async_copy(three, three, shared.at[2 * which + end]).wait()
+
     for step in plan()[0]:
         if step[0] == "send":
             copy(step[1]).start()
         elif step[0] == "product":
             product(step[1])
+        elif step[0] == "share":
+            share(dens, 0)
         elif step[0] == "weights":
             for table in tables:
                 table.wait()
@@ -353,20 +380,15 @@
         else:
             landed(step[1])
 
+    share(tails, 1)
+    shared_by_all(dens, 0)
+    density[...] = dens[0] + dens[1] + dens[2] + dens[3]
     for key in todo:
         copy(key).wait_send()
-    shares = [
-        pltpu.make_async_remote_copy(
-            src_ref=dens.at[orb], dst_ref=dens.at[orb], send_sem=shared.at[0], recv_sem=shared.at[1], device_id=peer, device_id_type=MESH
-        )
-        for peer in (device(at_x(2), y, z, core), device(at_x(2), y, z, 1 - core), to["d"])
-    ]
-    for share in shares:
-        share.start()
-    three = dens.at[pl.ds(0, 3)]
-    pltpu.make_async_copy(three, three, shared.at[1]).wait()
-    density[...] = dens[0] + dens[1] + dens[2] + dens[3]
-    pltpu.make_async_copy(three, three, shared.at[0]).wait()
+    shared_by_all(tails, 1)
+    last = tails[0] + tails[1] + tails[2] + tails[3]
+    for half in range(2):
+        density[1:2, pl.ds(half * 512 + TAIL, 512 - TAIL)] = last[half : half + 1]
 
 
 def write_out(held, held_density, rotated, density, sem):
@@ -397,11 +419,11 @@
             pltpu.VMEM((4, 1536, 256), jnp.bfloat16),
             pltpu.VMEM((2, 512 - TAIL, 128), jnp.float32),
             pltpu.VMEM((4, 2, 1024), jnp.float32),
+            pltpu.VMEM((4, 2, 512 - TAIL), jnp.float32),
             pltpu.SemaphoreType.DMA((n,)),
             pltpu.SemaphoreType.DMA((1,)),
-            pltpu.SemaphoreType.DMA((3,)),
             pltpu.SemaphoreType.DMA((4,)),
-            pltpu.SemaphoreType.DMA((2,)),
+            pltpu.SemaphoreType.DMA((4,)),
             pltpu.SemaphoreType.REGULAR,
         ],
         compiler_params=pltpu.CompilerParams(collective_id=0, has_side_effects=True, vmem_limit_bytes=VMEM_BYTES),

time: 65.5 us -> 63.6 us (0.971)
  Pallas kernels: 64.7 us -> 62.9 us
    pallas_call x1, Pallas kernels: 63.3 us -> 61.5 us  [local(): pl.pallas_call(kernel, out_shape=(pltpu.VMEM(*values), pltpu.VMEM(*sums))...]
where the time goes in v3:
time: 63.6 us; the launch traced here: 63.5 us
  Pallas kernels  62.9 us (99%)
  between operations  0.64 us (1%)
    pallas_call x1, Pallas kernels, local(): pl.pallas_call(kernel, out_shape=(pltpu.VMEM(*values), pltpu.VMEM(*sums))...  61.5 us
    pallas_call x1, Pallas kernels, local(): pl.pallas_call(write_out, out_shape=(jax.ShapeDtypeStruct(*values), jax.S...  1.39 us

profile of v3, /device:TPU:1, one launch (start us, length us, event | category | flops | bytes accessed | tf_op | source)
XLA Modules:
  0.0 63.5 jit_solution(9705150785893190876)
XLA Ops:
  0.6 61.5 %shard_map.77 = (bf16[2,4,2,512,128]{4,3,2,1,0:T(8,128)(2,1)S(1)}, f32[2,1024]{1,0:T(2,128)S(1)}) custom-call(s32[2,4]{1,0:T(2,128)} %ids_in.1, s32[2]{0:T(128)} %count_in.1, s32[3,16]{1,0:T(4,128)} %bitcast.6, bf16[48,8,128]{2,1,0:T(8,128)(2,1)} %bitcast.5, bf16[2,4,2,512,128]{4,3,2,1,0:T(8,128)(2,1)} %bitcast.4, f32[16,128]{1,0:T(8,128)} %occ_in.1), custom_call_target="tpu_custom_call" | custom-call | tf_op jit(solution)/shard_map/pallas_call | solution.py:407
  62.1 1.4 %shard_map.78 = (bf16[2,4,2,512,128]{4,3,2,1,0:T(8,128)(2,1)}, f32[2,1024]{1,0:T(2,128)}) custom-call(bf16[2,4,2,512,128]{4,3,2,1,0:T(8,128)(2,1)S(1)} %get-tuple-element.6.held, f32[2,1024]{1,0:T(2,128)S(1)} %get-tuple-element.7.held_density), custom_call_target="tpu_custom_call" | custom-call | tf_op jit(solution)/shard_map/pallas_call | solution.py:431

commit v4 on v3

--- a/solution.py
+++ b/solution.py
@@ -11,7 +11,7 @@
 MESH = pl.DeviceIdType.MESH
 NX, NY, NZ = 4, 4, 8
 TILES = 46
-A_TILES = 18
+A_TILES = 19
 VMEM_BYTES = 67043328 - 2097152 - 8192
 B_SETS = {1: (0, 1, -2, 3), -1: (-1, 2, -3, 4)}
 CHUNKS = [(0, 0, 256), (0, 256, 256), (1, 0, 128), (1, 128, 128), (1, 256, 128), (1, 384, 64), (1, 448, 32), (1, 480, 32)]
@@ -29,26 +29,44 @@
         out[key] = (link, size, needs, group or key)
 
     add(("swap",), "xs", a + b, [("tiles",)])
-    mine = [("swap",), ("z",)]
-    for n in range(1, 5):
+    half_of = {1: 0, -1: 1}
+    mine = [[("z",)], [("z",), ("swap",)]]
+    for n in range(1, 4):
+        for w in range(2):
+            for s in (1, -1):
+                add(("Bz", s, n, w), ("z", s), b, mine[w] if n == 1 else [("Bz", n - 1, w)], ("Bz", n, w))
+    for s in (1, -1):
+        add(("Bz", s, 4, half_of[s]), ("z", s), b, [("Bz", 3, half_of[s])], ("Bz4",))
+    for w in range(2):
         for s in (1, -1):
-            add(("Bz", s, n), ("z", s), 2 * b if n < 4 else b, mine if n == 1 else [("Bz", s, n - 1)], ("Bz4",) if n == 4 else None)
+            add(("Ay1", s, w), ("y", s), a, mine[w], ("Ay1", w))
     for s in (1, -1):
-        add(("Ay1", s), ("y", s), 2 * a, mine, ("Ay1",))
-        add(("Ay2", s), ("y", s), a, [("Ay1",)], ("Ay2",))
-    have_a = {0: mine, -1: [("Ay1",)], 1: [("Ay1",)], 2: [("Ay2",)]}
+        add(("Ay2", s, half_of[s]), ("y", s), a, [("Ay1", half_of[s])], ("Ay2",))
+    sides = [("Ay1", 0), ("Ay1", 1)]
+    have_a = {0: mine[1], -1: sides, 1: sides, 2: [("Ay2",)]}
     for dy in (0, -1, 1, 2):
         for n in range(1, 5):
             for s in (1, -1):
-                needs = have_a[dy] if n == 1 else [("Az", s, dy, n - 1)]
-                add(("Az", s, dy, n), ("z", s), 2 * a if n < 4 else a, needs, ("Az4",) if n == 4 else None)
-    have_b = {0: mine, 4: [("Bz4",)]}
+                before = [("Az", dy, n - 1)] if dy or n == 4 else [("Az", dy, n - 1, w) for w in range(2)]
+                if n == 4:
+                    add(("Az", s, dy, 4, half_of[s]), ("z", s), a, before, ("Az4",))
+                elif dy == 0 and n < 3:
+                    for w in range(2):
+                        add(("Az", s, dy, n, w), ("z", s), a, mine[w] if n == 1 else [("Az", dy, n - 1, w)], ("Az", dy, n, w))
+                else:
+                    add(("Az", s, dy, n), ("z", s), 2 * a, have_a[dy] if n == 1 else before, ("Az", dy, n))
+    have_b = {0: mine[1], 4: [("Bz4",)]}
     for n in range(1, 4):
-        have_b[-n], have_b[n] = [("Bz", 1, n)], [("Bz", -1, n)]
+        have_b[-n] = have_b[n] = [("Bz", n, 0), ("Bz", n, 1)]
     for dz in (0, -1, 1, -2, 2, -3, 3, 4):
         for s in (1, -1):
             onward = dz in B_SETS[s]
-            add(("By1", s, dz), ("y", s), 2 * b, have_b[dz], None if onward else ("By1", s))
+            group = ("By1", s, dz) if onward else ("By1", s)
+            if dz == 0:
+                for w in range(2):
+                    add(("By1", s, dz, w), ("y", s), b, mine[w], group)
+            else:
+                add(("By1", s, dz), ("y", s), 2 * b, have_b[dz], group)
             if onward:
                 add(("By2", s, dz), ("y", s), 2 * b, [("By1", s, dz)], ("By2",))
     row = 4 * 128 * 2
@@ -82,7 +100,7 @@
     @functools.lru_cache(None)
     def path(key):
         link, size, _, group = todo[key]
-        return size / rate.get(link, 45e3) + 1.9 + max([path(k) for k in after.get(group, [])], default=0)
+        return size / rate.get(link, 46.9e3) + 1.9 + max([path(k) for k in after.get(group, [])], default=0)
 
     free, here, due, order, pending = {}, set(), [], [], dict(todo)
     now = 0.0
@@ -97,14 +115,14 @@
             pending.pop(key)
             links = [("x", 1), ("x", -1)] if link == "xs" else [link]
             start = max([now] + [t for one in links for t in free.get(one, [])[-1:]])
-            end = start + size / rate.get(link, 45e3)
+            end = start + size / rate.get(link, 46.9e3)
             for one in links:
                 free.setdefault(one, []).append(end)
             heapq.heappush(due, (end + (1.0 if link == "d" else 1.9), len(order), key))
             order.append(("send", key))
 
     for i, group in enumerate([("tiles",), ("own", 0), ("own", 1), ("z",)]):
-        heapq.heappush(due, (3.0 if group == ("z",) else 0.01 * i, i - 50, group))
+        heapq.heappush(due, (0.5 if group == ("z",) else 0.01 * i, i - 50, group))
         left[group] = {group}
     tiles_left = {g for g in left if g[0] in ("tiles", "swap", "Bz", "Bz4", "Ay1", "Ay2", "Az", "Az4", "By1", "By2")}
     weights, done = False, 0
@@ -168,8 +186,8 @@
 
     A, B, BOTH, ALL = pl.ds(0, A_TILES), pl.ds(A_TILES, TILES - A_TILES), pl.ds(0, 2), slice(None)
 
-    def lows(s, half):
-        return pl.ds(0 if s > 0 else 1, 1) if half else BOTH
+    def low(w=None):
+        return BOTH if w is None else pl.ds(x_lo + w - 2 * w * x_lo, 1)
 
     def side(s):
         return 0 if s > 0 else 1
@@ -183,17 +201,17 @@
         if kind == "swap":
             return (T.at[z, y, x_lo],) * 2
         if kind == "Bz":
-            _, s, n = key
-            return (T.at[at_z(-(n - 1) * s), y, lows(s, n == 4), B],) * 2
+            _, s, n, w = key
+            return (T.at[at_z(-(n - 1) * s), y, low(w), B],) * 2
         if kind == "Ay1":
-            return (T.at[z, y, BOTH, A],) * 2
+            return (T.at[z, y, low(key[2]), A],) * 2
         if kind == "Ay2":
-            return (T.at[z, at_y(-key[1]), lows(key[1], True), A],) * 2
+            return (T.at[z, at_y(-key[1]), low(key[2]), A],) * 2
         if kind == "Az":
-            _, s, dy, n = key
-            return (T.at[at_z(-(n - 1) * s), at_y(dy), lows(s, n == 4), A],) * 2
+            s, dy, n = key[1:4]
+            return (T.at[at_z(-(n - 1) * s), at_y(dy), low(*key[4:]), A],) * 2
         if kind == "By1":
-            return (T.at[at_z(key[2]), y, BOTH, B],) * 2
+            return (T.at[at_z(key[2]), y, low(*key[3:]), B],) * 2
         if kind == "By2":
             return (T.at[at_z(key[2]), at_y(-key[1]), BOTH, B],) * 2
         if kind == "X1":
@@ -219,20 +237,25 @@
 
     def landed(group):
         kind = group[0]
-        if kind == "Bz4":
+        one, two = pl.ds(0, 1), pl.ds(0, 2)
+        if kind == "Bz":
+            where = T.at[two, y, one, B]
+        elif kind == "Bz4":
             where = T.at[z, y, BOTH, B]
         elif kind == "Ay1":
-            where = T.at[z, pl.ds(0, 2), BOTH, A]
+            where = T.at[z, two, one, A]
         elif kind == "Ay2":
             where = T.at[z, y, BOTH, A]
+        elif kind == "Az":
+            where = T.at[two, y, BOTH if len(group) == 3 else one, A]
+        elif kind == "Az4":
+            where = T.at[z, ALL, BOTH, A]
+        elif kind == "By1":
+            where = T.at[z, y, BOTH, B] if len(group) == 3 else T.at[pl.ds(0, 4), y, BOTH, B]
+        elif kind == "By2":
+            where = T.at[ALL, y, BOTH, B]
         elif kind == "X1":
             where = F.at[ALL, group[1] // 2, ALL, pl.ds(group[1] % 2 * 256, 256)]
-        elif kind == "Az4":
-            where = T.at[z, ALL, BOTH, A]
-        elif kind == "By1" and len(group) == 2:
-            where = T.at[pl.ds(0, 4), y, BOTH, B]
-        elif kind == "By2":
-            where = T.at[ALL, y, BOTH, B]
         elif kind == "X2":
             g, first, rows = CHUNKS[group[1]]
             where = X.at[far, g, ALL, ALL, pl.ds(first, rows)]

time: 63.6 us -> 62.2 us (0.978)
  Pallas kernels: 62.9 us -> 61.4 us
    pallas_call x1, Pallas kernels: 61.5 us -> 60 us  [local(): pl.pallas_call(kernel, out_shape=(pltpu.VMEM(*values), pltpu.VMEM(*sums))...]
where the time goes in v4:
time: 62.2 us; the launch traced here: 62.1 us
  Pallas kernels  61.4 us (99%)
  between operations  0.64 us (1%)
    pallas_call x1, Pallas kernels, local(): pl.pallas_call(kernel, out_shape=(pltpu.VMEM(*values), pltpu.VMEM(*sums))...  60 us
    pallas_call x1, Pallas kernels, local(): pl.pallas_call(write_out, out_shape=(jax.ShapeDtypeStruct(*values), jax.S...  1.39 us

profile of v4, /device:TPU:1, one launch (start us, length us, event | category | flops | bytes accessed | tf_op | source)
XLA Modules:
  0.0 62.1 jit_solution(15255638496372046624)
XLA Ops:
  0.6 60.0 %shard_map.77 = (bf16[2,4,2,512,128]{4,3,2,1,0:T(8,128)(2,1)S(1)}, f32[2,1024]{1,0:T(2,128)S(1)}) custom-call(s32[2,4]{1,0:T(2,128)} %ids_in.1, s32[2]{0:T(128)} %count_in.1, s32[3,16]{1,0:T(4,128)} %bitcast.6, bf16[48,8,128]{2,1,0:T(8,128)(2,1)} %bitcast.5, bf16[2,4,2,512,128]{4,3,2,1,0:T(8,128)(2,1)} %bitcast.4, f32[16,128]{1,0:T(8,128)} %occ_in.1), custom_call_target="tpu_custom_call" | custom-call | tf_op jit(solution)/shard_map/pallas_call | solution.py:430
  60.7 1.4 %shard_map.78 = (bf16[2,4,2,512,128]{4,3,2,1,0:T(8,128)(2,1)}, f32[2,1024]{1,0:T(2,128)}) custom-call(bf16[2,4,2,512,128]{4,3,2,1,0:T(8,128)(2,1)S(1)} %get-tuple-element.6.held, f32[2,1024]{1,0:T(2,128)S(1)} %get-tuple-element.7.held_density), custom_call_target="tpu_custom_call" | custom-call | tf_op jit(solution)/shard_map/pallas_call | solution.py:454

commit v5 on v4

--- a/solution.py
+++ b/solution.py
@@ -14,9 +14,10 @@
 A_TILES = 19
 VMEM_BYTES = 67043328 - 2097152 - 8192
 B_SETS = {1: (0, 1, -2, 3), -1: (-1, 2, -3, 4)}
-CHUNKS = [(0, 0, 256), (0, 256, 256), (1, 0, 128), (1, 128, 128), (1, 256, 128), (1, 384, 64), (1, 448, 32), (1, 480, 32)]
-UNITS = [(0, 0, 256), (0, 256, 256), (1, 0, 256), (1, 256, 128), (1, 384, 64), (1, 448, 32), (1, 480, 32)]
+CHUNKS = [(0, 0, 256), (0, 256, 256), (1, 0, 128), (1, 128, 128), (1, 256, 128), (1, 384, 64), (1, 448, 48), (1, 496, 16)]
+UNITS = [(0, 0, 256), (0, 256, 256), (1, 0, 256), (1, 256, 128), (1, 384, 64), (1, 448, 64)]
 TAIL = 384
+DIRECT = len(CHUNKS) - 1
 DEPTH = 2
 
 
@@ -77,7 +78,10 @@
     for k, (g, first, rows) in enumerate(CHUNKS):
         for s in (1, -1):
             add(("X2", s, k), ("x", s), rows * row, [("X1", g * 2 + first // 256)], ("X2", k))
-        add(("Xd", k), "d", 2 * rows * row, [("X2", k)])
+            if k == DIRECT:
+                add(("X2c", s, k), ("x", s), rows * row, [("X1", g * 2 + first // 256)], ("X2", k))
+        if k < DIRECT:
+            add(("Xd", k), "d", 2 * rows * row, [("X2", k)])
     return out
 
 
@@ -139,8 +143,9 @@
             continue
         ready = weights and done < len(UNITS) and ("Od",) in here
         if ready:
-            ready = all((t, k) in here for t in ("X2", "Xd") for k in chunks_of(done)) and all(("X2", k) in here for k in chunks_of(done + 1))
-        if not weights and not tiles_left:
+            ready = all((t, k) in here for t in ("X2", "Xd") for k in chunks_of(done) if (t, k) in left)
+            ready = ready and all(("X2", k) in here for k in chunks_of(done + 1) if k < DIRECT)
+        if not weights and not tiles_left and ("X2", 2) in here:
             order.append(("weights",))
             weights = True
             now += 0.7
@@ -153,12 +158,20 @@
         else:
             now = due[0][0]
     assert not pending
-    return order, now
+    late = [("wait", group) for group in left if group[0] in ("Od", "Xd")]
+    out = []
+    for step in order:
+        if step[0] == "product":
+            out += [("wait", ("Od",))] * (step[1] == 0) + [("begin", step[1])] * (step[1] == len(UNITS) - 1)
+            out += [("wait", ("Xd", k)) for k in chunks_of(step[1]) if k < DIRECT]
+        if step not in late:
+            out.append(step)
+    return out, now
 
 
 def kernel(
     ids_in, count_in, pattern_in, band, orbitals, occ_in, rotated, density,
-    ids, count, pattern, occ, T, X, F, W, D, dens, tails, recv, sent, local, shared, ready,
+    ids, count, pattern, occ, T, X, F, W, D, E, dens, tails, recv, sent, local, shared, ready,
 ):
     dom, orb = lax.axis_index("dom"), lax.axis_index("orb")
     x_lo, z, y = lax.div(dom, 32), lax.rem(lax.div(dom, 4), 8), lax.rem(dom, 4)
@@ -218,7 +231,7 @@
             _, s, i = key
             rows = pl.ds(i % 2 * 256, 256)
             return X.at[orb, i // 2, ALL, side(s), rows], F.at[side(s), i // 2, ALL, rows]
-        if kind == "X2":
+        if kind in ("X2", "X2c"):
             _, s, k = key
             g, first, rows = CHUNKS[k]
             source = lax.div(at_x(-s), 2) * 2 + core
@@ -232,7 +245,7 @@
         src, dst = ends(key)
         return pltpu.make_async_remote_copy(
             src_ref=src, dst_ref=dst, send_sem=sent.at[0], recv_sem=recv.at[number[todo[key][3]]],
-            device_id=to[todo[key][0]], device_id_type=MESH,
+            device_id=device(at_x(key[1]), y, z, 1 - core) if key[0] == "X2c" else to[todo[key][0]], device_id_type=MESH,
         )
 
     def landed(group):
@@ -258,7 +271,8 @@
             where = F.at[ALL, group[1] // 2, ALL, pl.ds(group[1] % 2 * 256, 256)]
         elif kind == "X2":
             g, first, rows = CHUNKS[group[1]]
-            where = X.at[far, g, ALL, ALL, pl.ds(first, rows)]
+            orbs = pl.ds(lax.div(at_x(2), 2) * 2, 2) if group[1] == DIRECT else far
+            where = X.at[orbs, g, ALL, ALL, pl.ds(first, rows)]
         else:
             where = ends(group)[1]
         pltpu.make_async_copy(where, where, recv.at[number[group]]).wait()
@@ -303,19 +317,32 @@
             (((1,), (1,)), ((), ())), preferred_element_type=jnp.float32,
         )
 
+    def multiply(u, pair, orbs):
+        g, first, n = UNITS[u]
+        parts = [(at, q) for at in range(3) for q in orbs]
+        values = jnp.concatenate(
+            [jnp.concatenate([X[q, g, pair + at, half, pl.ds(first, n)] for at, q in parts], axis=1) for half in range(2)], axis=0
+        )
+        if len(orbs) == 4:
+            tiles = W[g * 2 + pair]
+        else:
+            tiles = jnp.concatenate([W[g * 2 + pair, pl.ds(pl.multiple_of(at * 512 + q * 128, 128), 128)] for at, q in parts], axis=0)
+        return jnp.dot(values, tiles, preferred_element_type=jnp.float32)
+
+    def begin(u):
+        for pair in range(2):
+            E[pair] = multiply(u, pair, (orb, x_hi * 2 + 1 - core, far))
+
     def product(u):
         g, first, n = UNITS[u]
         rows = pl.ds(first, n)
         total = jnp.zeros((2 * n, 128), jnp.float32)
         for pair in range(2):
-            values = jnp.concatenate(
-                [
-                    jnp.concatenate([X[q, g, pair + at, half, rows] for at in range(3) for q in range(4)], axis=1)
-                    for half in range(2)
-                ],
-                axis=0,
-            )
-            out = jnp.dot(values, W[g * 2 + pair], preferred_element_type=jnp.float32).astype(jnp.bfloat16)
+            if u < len(UNITS) - 1:
+                out = multiply(u, pair, range(4))
+            else:
+                out = E[pair] + multiply(u, pair, (lax.div(at_x(2), 2) * 2 + 1 - core,))
+            out = out.astype(jnp.bfloat16)
             for which in range(2):
                 m = pair * 2 + which
                 one = out[:, which * 128 : which * 128 + 128]
@@ -338,25 +365,25 @@
         for half in range(2):
             dens[orb, pl.ds(g, 1), pl.ds(half * 512 + first, n)] = summed[0:1, half * n : half * n + n]
 
+    barrier = pltpu.get_barrier_semaphore()
+    for step in (1, -1):
+        pl.semaphore_signal(barrier, inc=1, device_id=device(at_x(step), y, z, 0), device_id_type=MESH)
+    for step in (1, -1):
+        pl.semaphore_signal(barrier, inc=1, device_id=device(x, at_y(step), z, 1), device_id_type=MESH)
+        pl.semaphore_signal(barrier, inc=1, device_id=device(x, y, at_z(step), 1), device_id_type=MESH)
+
+    @pl.when(core == 1)
+    def _():
+        pl.semaphore_signal(barrier, inc=1, device_id=device(x, y, z, 0), device_id_type=MESH)
+
     for load in loads.values():
         load.start()
     for table in tables:
         table.start()
 
-    barrier = pltpu.get_barrier_semaphore()
-    for step in (1, -1, 2):
-        pl.semaphore_signal(barrier, inc=1, device_id=device(at_x(step), y, z, 0), device_id_type=MESH)
-    for step in (1, -1):
-        pl.semaphore_signal(barrier, inc=1, device_id=device(x, at_y(step), z, 1), device_id_type=MESH)
-        pl.semaphore_signal(barrier, inc=1, device_id=device(x, y, at_z(step), 1), device_id_type=MESH)
-
-    @pl.when(core == 1)
-    def _():
-        pl.semaphore_signal(barrier, inc=1, device_id=device(x, y, z, 0), device_id_type=MESH)
-
     @pl.when(core == 0)
     def _():
-        pl.semaphore_wait(barrier, 7)
+        pl.semaphore_wait(barrier, 5)
         pl.semaphore_signal(ready, inc=1, device_id=device(x, y, z, 1), device_id_type=MESH)
 
     @pl.when(core == 1)
@@ -390,6 +417,8 @@
             copy(step[1]).start()
         elif step[0] == "product":
             product(step[1])
+        elif step[0] == "begin":
+            begin(step[1])
         elif step[0] == "share":
             share(dens, 0)
         elif step[0] == "weights":
@@ -441,6 +470,7 @@
             pltpu.VMEM((2, 2, 4, 512, 128), jnp.bfloat16),
             pltpu.VMEM((4, 1536, 256), jnp.bfloat16),
             pltpu.VMEM((2, 512 - TAIL, 128), jnp.float32),
+            pltpu.VMEM((2, 2 * UNITS[-1][2], 256), jnp.float32),
             pltpu.VMEM((4, 2, 1024), jnp.float32),
             pltpu.VMEM((4, 2, 512 - TAIL), jnp.float32),
             pltpu.SemaphoreType.DMA((n,)),

time: 62.2 us -> 61.2 us (0.984)
  Pallas kernels: 61.4 us -> 60.5 us
    pallas_call x1, Pallas kernels: 60 us -> 59.1 us  [local(): pl.pallas_call(kernel, out_shape=(pltpu.VMEM(*values), pltpu.VMEM(*sums))...]
where the time goes in v5:
time: 61.2 us; the launch traced here: 61.1 us
  Pallas kernels  60.5 us (99%)
  between operations  0.64 us (1%)
    pallas_call x1, Pallas kernels, local(): pl.pallas_call(kernel, out_shape=(pltpu.VMEM(*values), pltpu.VMEM(*sums))...  59.1 us
    pallas_call x1, Pallas kernels, local(): pl.pallas_call(write_out, out_shape=(jax.ShapeDtypeStruct(*values), jax.S...  1.39 us

profile of v5, /device:TPU:1, one launch (start us, length us, event | category | flops | bytes accessed | tf_op | source)
XLA Modules:
  0.0 61.1 jit_solution(2927716332810546681)
XLA Ops:
  0.6 59.1 %shard_map.77 = (bf16[2,4,2,512,128]{4,3,2,1,0:T(8,128)(2,1)S(1)}, f32[2,1024]{1,0:T(2,128)S(1)}) custom-call(s32[2,4]{1,0:T(2,128)} %ids_in.1, s32[2]{0:T(128)} %count_in.1, s32[3,16]{1,0:T(4,128)} %bitcast.6, bf16[48,8,128]{2,1,0:T(8,128)(2,1)} %bitcast.5, bf16[2,4,2,512,128]{4,3,2,1,0:T(8,128)(2,1)} %bitcast.4, f32[16,128]{1,0:T(8,128)} %occ_in.1), custom_call_target="tpu_custom_call" | custom-call | tf_op jit(solution)/shard_map/pallas_call | solution.py:459
  59.7 1.4 %shard_map.78 = (bf16[2,4,2,512,128]{4,3,2,1,0:T(8,128)(2,1)}, f32[2,1024]{1,0:T(2,128)}) custom-call(bf16[2,4,2,512,128]{4,3,2,1,0:T(8,128)(2,1)S(1)} %get-tuple-element.6.held, f32[2,1024]{1,0:T(2,128)S(1)} %get-tuple-element.7.held_density), custom_call_target="tpu_custom_call" | custom-call | tf_op jit(solution)/shard_map/pallas_call | solution.py:484

commit v6 on v5

--- a/solution.py
+++ b/solution.py
@@ -11,14 +11,15 @@
 MESH = pl.DeviceIdType.MESH
 NX, NY, NZ = 4, 4, 8
 TILES = 46
-A_TILES = 19
+A_TILES = 18
 VMEM_BYTES = 67043328 - 2097152 - 8192
 B_SETS = {1: (0, 1, -2, 3), -1: (-1, 2, -3, 4)}
 CHUNKS = [(0, 0, 256), (0, 256, 256), (1, 0, 128), (1, 128, 128), (1, 256, 128), (1, 384, 64), (1, 448, 48), (1, 496, 16)]
 UNITS = [(0, 0, 256), (0, 256, 256), (1, 0, 256), (1, 256, 128), (1, 384, 64), (1, 448, 64)]
 TAIL = 384
+SHARED = 4
 DIRECT = len(CHUNKS) - 1
-DEPTH = 2
+DEPTH = 3
 
 
 def messages():
@@ -74,7 +75,7 @@
     for i in range(4):
         for s in (1, -1):
             add(("X1", s, i), ("x", s), 256 * row, [("own", i // 2)], ("X1", i))
-    add(("Od",), "d", 2048 * row, [("own", 0), ("own", 1)])
+    add(("Od",), "d", 2048 * row, [("own", 0), ("own", 1), ("z",)])
     for k, (g, first, rows) in enumerate(CHUNKS):
         for s in (1, -1):
             add(("X2", s, k), ("x", s), rows * row, [("X1", g * 2 + first // 256)], ("X2", k))
@@ -128,45 +129,27 @@
     for i, group in enumerate([("tiles",), ("own", 0), ("own", 1), ("z",)]):
         heapq.heappush(due, (0.5 if group == ("z",) else 0.01 * i, i - 50, group))
         left[group] = {group}
-    tiles_left = {g for g in left if g[0] in ("tiles", "swap", "Bz", "Bz4", "Ay1", "Ay2", "Az", "Az4", "By1", "By2")}
-    weights, done = False, 0
-    while due or done < len(UNITS):
-        if due and due[0][0] <= now:
-            key = heapq.heappop(due)[2]
-            group = todo[key][3] if key in todo else key
-            left[group].discard(key)
-            if not left[group]:
-                order.append(("wait", group))
-                here.add(group)
-                tiles_left.discard(group)
-            send_ready()
+    first = {g for g in left if g[0] not in ("X2", "Xd", "Od")} | {("X2", 0)}
+    while not first <= here:
+        now = max(now, due[0][0])
+        key = heapq.heappop(due)[2]
+        group = todo[key][3] if key in todo else key
+        left[group].discard(key)
+        if left[group] or group not in first:
             continue
-        ready = weights and done < len(UNITS) and ("Od",) in here
-        if ready:
-            ready = all((t, k) in here for t in ("X2", "Xd") for k in chunks_of(done) if (t, k) in left)
-            ready = ready and all(("X2", k) in here for k in chunks_of(done + 1) if k < DIRECT)
-        if not weights and not tiles_left and ("X2", 2) in here:
-            order.append(("weights",))
-            weights = True
-            now += 0.7
-        elif ready:
-            if UNITS[done][:2] == (1, TAIL):
-                order.append(("share",))
-            order.append(("product", done))
-            now += 0.4 + 0.4 * UNITS[done][2] / 128
-            done += 1
-        else:
-            now = due[0][0]
-    assert not pending
-    late = [("wait", group) for group in left if group[0] in ("Od", "Xd")]
-    out = []
-    for step in order:
-        if step[0] == "product":
-            out += [("wait", ("Od",))] * (step[1] == 0) + [("begin", step[1])] * (step[1] == len(UNITS) - 1)
-            out += [("wait", ("Xd", k)) for k in chunks_of(step[1]) if k < DIRECT]
-        if step not in late:
-            out.append(step)
-    return out, now
+        order.append(("wait", group))
+        here.add(group)
+        send_ready()
+
+    def forward(*chunks):
+        return [step for k in chunks for step in [("wait", ("X2", k))] + [("send", ("Xd", k))] * (k < DIRECT)]
+
+    def product(u):
+        return [("wait", ("Xd", k)) for k in chunks_of(u) if k < DIRECT] + [("product", u)]
+
+    order += forward(1) + [("weights",), ("wait", ("Od",))] + forward(2) + product(0) + forward(3) + product(1)
+    order += forward(4) + product(2) + forward(5) + product(3) + forward(6) + product(4) + [("share",)] + forward(DIRECT) + [("begin", 5)] + product(5)
+    return order
 
 
 def kernel(
@@ -307,15 +290,11 @@
                             rows = T[:, :, low, t].astype(jnp.float32).reshape(256, 128) * scale
                             W[g * 2 + pair, pl.ds(at * 512 + low * 256, 256), columns] = rows.astype(jnp.bfloat16)
 
-    def lane_sums(total):
-        high = total.astype(jnp.bfloat16)
-        rest = total - high.astype(jnp.float32)
-        middle = rest.astype(jnp.bfloat16)
-        low = (rest - middle.astype(jnp.float32)).astype(jnp.bfloat16)
-        return lax.dot_general(
-            jnp.ones((8, 384), jnp.bfloat16), jnp.concatenate([high, middle, low], axis=1),
-            (((1,), (1,)), ((), ())), preferred_element_type=jnp.float32,
-        )
+    def lane_sums(u):
+        g, first, n = UNITS[u]
+        for half in range(2):
+            total = D[g, half, pl.ds(first, n)]
+            dens[orb, pl.ds(g, 1), pl.ds(half * 512 + first, n)] = jnp.sum(total.T, axis=0, keepdims=True)
 
     def multiply(u, pair, orbs):
         g, first, n = UNITS[u]
@@ -350,27 +329,20 @@
                     rotated[g, m, half, rows] = one[half * n : half * n + n]
                 wide = one.astype(jnp.float32)
                 total = total + wide * wide * occ[pl.ds(ids[g, m], 1), :]
-        tail = g == 1 and first >= TAIL
-        if tail:
+        for half in range(2):
+            D[g, half, rows] = total[half * n : half * n + n]
+        if 1 <= u <= SHARED:
+            lane_sums(u - 1)
+        if u == len(UNITS) - 1:
             for half in range(2):
-                D[half, pl.ds(first - TAIL, n)] = total[half * n : half * n + n]
-            if u < len(UNITS) - 1:
-                return
-            n = 512 - TAIL
-            summed = lane_sums(D[...].reshape(2 * n, 128))
-            for half in range(2):
-                tails[orb, pl.ds(half, 1)] = summed[0:1, half * n : half * n + n]
-            return
-        summed = lane_sums(total)
-        for half in range(2):
-            dens[orb, pl.ds(g, 1), pl.ds(half * 512 + first, n)] = summed[0:1, half * n : half * n + n]
+                tails[orb, pl.ds(half, 1)] = jnp.sum(D[1, half, pl.ds(TAIL, 512 - TAIL)].T, axis=0, keepdims=True)
 
     barrier = pltpu.get_barrier_semaphore()
     for step in (1, -1):
-        pl.semaphore_signal(barrier, inc=1, device_id=device(at_x(step), y, z, 0), device_id_type=MESH)
+        pl.semaphore_signal(barrier, inc=1, device_id=to["x", step], device_id_type=MESH)
     for step in (1, -1):
-        pl.semaphore_signal(barrier, inc=1, device_id=device(x, at_y(step), z, 1), device_id_type=MESH)
-        pl.semaphore_signal(barrier, inc=1, device_id=device(x, y, at_z(step), 1), device_id_type=MESH)
+        pl.semaphore_signal(barrier, inc=1, device_id=device(x, at_y(step), z, 0), device_id_type=MESH)
+        pl.semaphore_signal(barrier, inc=1, device_id=device(x, y, at_z(step), 0), device_id_type=MESH)
 
     @pl.when(core == 1)
     def _():
@@ -383,20 +355,15 @@
 
     @pl.when(core == 0)
     def _():
-        pl.semaphore_wait(barrier, 5)
+        pl.semaphore_wait(barrier, 11)
         pl.semaphore_signal(ready, inc=1, device_id=device(x, y, z, 1), device_id_type=MESH)
 
     @pl.when(core == 1)
     def _():
-        pl.semaphore_wait(ready, 1)
+        pl.semaphore_wait(barrier, 2)
 
     def neighbours():
         @pl.when(core == 1)
-        def _():
-            pl.semaphore_wait(barrier, 8)
-            pl.semaphore_signal(ready, inc=1, device_id=device(x, y, z, 0), device_id_type=MESH)
-
-        @pl.when(core == 0)
         def _():
             pl.semaphore_wait(ready, 1)
 
@@ -412,7 +379,7 @@
             three = sums.at[pl.ds(0, 3)]
             pltpu.make_async_copy(three, three, shared.at[2 * which + end]).wait()
 
-    for step in plan()[0]:
+    for step in plan():
         if step[0] == "send":
             copy(step[1]).start()
         elif step[0] == "product":
@@ -469,7 +436,7 @@
             pltpu.VMEM((4, 2, 4, 2, 512, 128), jnp.bfloat16),
             pltpu.VMEM((2, 2, 4, 512, 128), jnp.bfloat16),
             pltpu.VMEM((4, 1536, 256), jnp.bfloat16),
-            pltpu.VMEM((2, 512 - TAIL, 128), jnp.float32),
+            pltpu.VMEM((2, 2, 512, 128), jnp.float32),
             pltpu.VMEM((2, 2 * UNITS[-1][2], 256), jnp.float32),
             pltpu.VMEM((4, 2, 1024), jnp.float32),
             pltpu.VMEM((4, 2, 512 - TAIL), jnp.float32),

time: 61.2 us -> 60.4 us (0.987)
  Pallas kernels: 60.5 us -> 59.6 us
    pallas_call x1, Pallas kernels: 59.1 us -> 58.3 us  [local(): pl.pallas_call(kernel, out_shape=(pltpu.VMEM(*values), pltpu.VMEM(*sums))...]
where the time goes in v6:
time: 60.4 us; the launch traced here: 60.3 us
  Pallas kernels  59.6 us (99%)
  between operations  0.64 us (1%)
    pallas_call x1, Pallas kernels, local(): pl.pallas_call(kernel, out_shape=(pltpu.VMEM(*values), pltpu.VMEM(*sums))...  58.3 us
    pallas_call x1, Pallas kernels, local(): pl.pallas_call(write_out, out_shape=(jax.ShapeDtypeStruct(*values), jax.S...  1.39 us

profile of v6, /device:TPU:1, one launch (start us, length us, event | category | flops | bytes accessed | tf_op | source)
XLA Modules:
  0.0 60.3 jit_solution(7869096970455117159)
XLA Ops:
  0.6 58.3 %shard_map.77 = (bf16[2,4,2,512,128]{4,3,2,1,0:T(8,128)(2,1)S(1)}, f32[2,1024]{1,0:T(2,128)S(1)}) custom-call(s32[2,4]{1,0:T(2,128)} %ids_in.1, s32[2]{0:T(128)} %count_in.1, s32[3,16]{1,0:T(4,128)} %bitcast.6, bf16[48,8,128]{2,1,0:T(8,128)(2,1)} %bitcast.5, bf16[2,4,2,512,128]{4,3,2,1,0:T(8,128)(2,1)} %bitcast.4, f32[16,128]{1,0:T(8,128)} %occ_in.1), custom_call_target="tpu_custom_call" | custom-call | tf_op jit(solution)/shard_map/pallas_call | solution.py:426
  58.9 1.4 %shard_map.78 = (bf16[2,4,2,512,128]{4,3,2,1,0:T(8,128)(2,1)}, f32[2,1024]{1,0:T(2,128)}) custom-call(bf16[2,4,2,512,128]{4,3,2,1,0:T(8,128)(2,1)S(1)} %get-tuple-element.6.held, f32[2,1024]{1,0:T(2,128)S(1)} %get-tuple-element.7.held_density), custom_call_target="tpu_custom_call" | custom-call | tf_op jit(solution)/shard_map/pallas_call | solution.py:451

commit v7 on v6

--- a/solution.py
+++ b/solution.py
@@ -20,6 +20,10 @@
 SHARED = 4
 DIRECT = len(CHUNKS) - 1
 DEPTH = 3
+COMPUTE = (
+    ("s1", "w", "p0", "s2", "p1", "s3", "p2", "s4", "s5", "p3", "s6", "p4", "d", "s7", "b5", "p5"),
+    ("s1", "s2", "w", "p0", "s3", "p1", "s4", "s5", "s6", "p2", "p3", "p4", "d", "s7", "b5", "p5"),
+)
 
 
 def messages():
@@ -147,9 +151,19 @@
     def product(u):
         return [("wait", ("Xd", k)) for k in chunks_of(u) if k < DIRECT] + [("product", u)]
 
-    order += forward(1) + [("weights",), ("wait", ("Od",))] + forward(2) + product(0) + forward(3) + product(1)
-    order += forward(4) + product(2) + forward(5) + product(3) + forward(6) + product(4) + [("share",)] + forward(DIRECT) + [("begin", 5)] + product(5)
-    return order
+    def expand(steps):
+        out = []
+        for name in steps:
+            kind, i = name[0], int(name[1:] or 0)
+            if kind == "s":
+                out += forward(i)
+            elif kind == "p":
+                out += [("wait", ("Od",))] * (i == 0) + product(i)
+            else:
+                out.append(({"w": "weights", "b": "begin", "d": "share"}[kind], i))
+        return out
+
+    return order, [expand(steps) for steps in COMPUTE]
 
 
 def kernel(
@@ -379,25 +393,34 @@
             three = sums.at[pl.ds(0, 3)]
             pltpu.make_async_copy(three, three, shared.at[2 * which + end]).wait()
 
-    for step in plan():
-        if step[0] == "send":
-            copy(step[1]).start()
-        elif step[0] == "product":
-            product(step[1])
-        elif step[0] == "begin":
-            begin(step[1])
-        elif step[0] == "share":
-            share(dens, 0)
-        elif step[0] == "weights":
-            for table in tables:
-                table.wait()
-            weights()
-        elif step[1] in loads:
-            loads[step[1]].wait()
-        elif step[1] == ("z",):
-            neighbours()
-        else:
-            landed(step[1])
+    def run(steps):
+        for step in steps:
+            if step[0] == "send":
+                copy(step[1]).start()
+            elif step[0] == "product":
+                product(step[1])
+            elif step[0] == "begin":
+                begin(step[1])
+            elif step[0] == "share":
+                share(dens, 0)
+            elif step[0] == "weights":
+                for table in tables:
+                    table.wait()
+                weights()
+            elif step[1] in loads:
+                loads[step[1]].wait()
+            elif step[1] == ("z",):
+                neighbours()
+            else:
+                landed(step[1])
+
+    order, by_core = plan()
+    run(order)
+    if by_core[0] == by_core[1]:
+        run(by_core[0])
+    else:
+        for which in range(2):
+            pl.when(core == which)(functools.partial(run, by_core[which]))
 
     share(tails, 1)
     shared_by_all(dens, 0)

time: 60.4 us -> 59.7 us (0.988)
    pallas_call x1, Pallas kernels: 58.3 us -> 57.6 us  [local(): pl.pallas_call(kernel, out_shape=(pltpu.VMEM(*values), pltpu.VMEM(*sums))...]
where the time goes in v7:
time: 59.7 us; the launch traced here: 59.6 us
  Pallas kernels  59 us (99%)
  between operations  0.64 us (1%)
    pallas_call x1, Pallas kernels, local(): pl.pallas_call(kernel, out_shape=(pltpu.VMEM(*values), pltpu.VMEM(*sums))...  57.6 us
    pallas_call x1, Pallas kernels, local(): pl.pallas_call(write_out, out_shape=(jax.ShapeDtypeStruct(*values), jax.S...  1.39 us

profile of v7, /device:TPU:1, one launch (start us, length us, event | category | flops | bytes accessed | tf_op | source)
XLA Modules:
  0.0 59.6 jit_solution(13454311784728151282)
XLA Ops:
  0.6 57.6 %shard_map.77 = (bf16[2,4,2,512,128]{4,3,2,1,0:T(8,128)(2,1)S(1)}, f32[2,1024]{1,0:T(2,128)S(1)}) custom-call(s32[2,4]{1,0:T(2,128)} %ids_in.1, s32[2]{0:T(128)} %count_in.1, s32[3,16]{1,0:T(4,128)} %bitcast.6, bf16[48,8,128]{2,1,0:T(8,128)(2,1)} %bitcast.5, bf16[2,4,2,512,128]{4,3,2,1,0:T(8,128)(2,1)} %bitcast.4, f32[16,128]{1,0:T(8,128)} %occ_in.1), custom_call_target="tpu_custom_call" | custom-call | tf_op jit(solution)/shard_map/pallas_call | solution.py:449
  58.2 1.4 %shard_map.78 = (bf16[2,4,2,512,128]{4,3,2,1,0:T(8,128)(2,1)}, f32[2,1024]{1,0:T(2,128)}) custom-call(bf16[2,4,2,512,128]{4,3,2,1,0:T(8,128)(2,1)S(1)} %get-tuple-element.6.held, f32[2,1024]{1,0:T(2,128)S(1)} %get-tuple-element.7.held_density), custom_call_target="tpu_custom_call" | custom-call | tf_op jit(solution)/shard_map/pallas_call | solution.py:474

commit v8 on v7

--- a/solution.py
+++ b/solution.py
@@ -14,15 +14,15 @@
 A_TILES = 18
 VMEM_BYTES = 67043328 - 2097152 - 8192
 B_SETS = {1: (0, 1, -2, 3), -1: (-1, 2, -3, 4)}
-CHUNKS = [(0, 0, 256), (0, 256, 256), (1, 0, 128), (1, 128, 128), (1, 256, 128), (1, 384, 64), (1, 448, 48), (1, 496, 16)]
+CHUNKS = [(0, 0, 256), (0, 256, 256), (1, 0, 128), (1, 128, 128), (1, 256, 128), (1, 384, 64), (1, 448, 64)]
 UNITS = [(0, 0, 256), (0, 256, 256), (1, 0, 256), (1, 256, 128), (1, 384, 64), (1, 448, 64)]
 TAIL = 384
 SHARED = 4
-DIRECT = len(CHUNKS) - 1
+DIRECT = len(CHUNKS)
 DEPTH = 3
 COMPUTE = (
-    ("s1", "w", "p0", "s2", "p1", "s3", "p2", "s4", "s5", "p3", "s6", "p4", "d", "s7", "b5", "p5"),
-    ("s1", "s2", "w", "p0", "s3", "p1", "s4", "s5", "s6", "p2", "p3", "p4", "d", "s7", "b5", "p5"),
+    ("s1", "w", "p0", "s2", "p1", "s3", "p2", "s4", "s5", "p3", "s6", "p4", "d", "b5", "p5"),
+    ("s1", "s2", "w", "p0", "s3", "p1", "s4", "s5", "s6", "p2", "p3", "p4", "d", "b5", "p5"),
 )
 
 
@@ -76,15 +76,15 @@
             if onward:
                 add(("By2", s, dz), ("y", s), 2 * b, [("By1", s, dz)], ("By2",))
     row = 4 * 128 * 2
-    for i in range(4):
+    for i in range(2):
         for s in (1, -1):
-            add(("X1", s, i), ("x", s), 256 * row, [("own", i // 2)], ("X1", i))
+            add(("X1", s, i), ("x", s), 512 * row, [("own", i)], ("X1", i))
     add(("Od",), "d", 2048 * row, [("own", 0), ("own", 1), ("z",)])
     for k, (g, first, rows) in enumerate(CHUNKS):
         for s in (1, -1):
-            add(("X2", s, k), ("x", s), rows * row, [("X1", g * 2 + first // 256)], ("X2", k))
+            add(("X2", s, k), ("x", s), rows * row, [("X1", g)], ("X2", k))
             if k == DIRECT:
-                add(("X2c", s, k), ("x", s), rows * row, [("X1", g * 2 + first // 256)], ("X2", k))
+                add(("X2c", s, k), ("x", s), rows * row, [("X1", g)], ("X2", k))
         if k < DIRECT:
             add(("Xd", k), "d", 2 * rows * row, [("X2", k)])
     return out
@@ -226,8 +226,7 @@
             return (T.at[at_z(key[2]), at_y(-key[1]), BOTH, B],) * 2
         if kind == "X1":
             _, s, i = key
-            rows = pl.ds(i % 2 * 256, 256)
-            return X.at[orb, i // 2, ALL, side(s), rows], F.at[side(s), i // 2, ALL, rows]
+            return X.at[orb, i, ALL, side(s)], F.at[side(s), i]
         if kind in ("X2", "X2c"):
             _, s, k = key
             g, first, rows = CHUNKS[k]
@@ -265,7 +264,7 @@
         elif kind == "By2":
             where = T.at[ALL, y, BOTH, B]
         elif kind == "X1":
-            where = F.at[ALL, group[1] // 2, ALL, pl.ds(group[1] % 2 * 256, 256)]
+            where = F.at[ALL, group[1]]
         elif kind == "X2":
             g, first, rows = CHUNKS[group[1]]
             orbs = pl.ds(lax.div(at_x(2), 2) * 2, 2) if group[1] == DIRECT else far

time: 59.7 us -> 59.7 us (level)
  no operation moved by 1% of the time
where the time goes in v8:
time: 59.7 us; the launch traced here: 59.6 us
  Pallas kernels  58.9 us (99%)
  between operations  0.64 us (1%)
    pallas_call x1, Pallas kernels, local(): pl.pallas_call(kernel, out_shape=(pltpu.VMEM(*values), pltpu.VMEM(*sums))...  57.5 us
    pallas_call x1, Pallas kernels, local(): pl.pallas_call(write_out, out_shape=(jax.ShapeDtypeStruct(*values), jax.S...  1.39 us

profile of v8, /device:TPU:1, one launch (start us, length us, event | category | flops | bytes accessed | tf_op | source)
XLA Modules:
  0.0 59.6 jit_solution(4432111745022428607)
XLA Ops:
  0.6 57.5 %shard_map.77 = (bf16[2,4,2,512,128]{4,3,2,1,0:T(8,128)(2,1)S(1)}, f32[2,1024]{1,0:T(2,128)S(1)}) custom-call(s32[2,4]{1,0:T(2,128)} %ids_in.1, s32[2]{0:T(128)} %count_in.1, s32[3,16]{1,0:T(4,128)} %bitcast.6, bf16[48,8,128]{2,1,0:T(8,128)(2,1)} %bitcast.5, bf16[2,4,2,512,128]{4,3,2,1,0:T(8,128)(2,1)} %bitcast.4, f32[16,128]{1,0:T(8,128)} %occ_in.1), custom_call_target="tpu_custom_call" | custom-call | tf_op jit(solution)/shard_map/pallas_call | solution.py:448
  58.2 1.4 %shard_map.78 = (bf16[2,4,2,512,128]{4,3,2,1,0:T(8,128)(2,1)}, f32[2,1024]{1,0:T(2,128)}) custom-call(bf16[2,4,2,512,128]{4,3,2,1,0:T(8,128)(2,1)S(1)} %get-tuple-element.6.held, f32[2,1024]{1,0:T(2,128)S(1)} %get-tuple-element.7.held_density), custom_call_target="tpu_custom_call" | custom-call | tf_op jit(solution)/shard_map/pallas_call | solution.py:473
